TPU v7x, 32 devices: a 4x4x1 block of a 4x4x8 slice. The times are simulated.
32 devices in a mesh: pair: 1 (over z), tp: 4 (over y), node: 8 (over x, core).
Axes of the slice: x: 4, y: 4, z: 1, core: 2. Of those that a mesh axis runs over, the one named last changes fastest.
The devices are a block of a 4x4x8 slice.
Arguments:
- prompt: bfloat16 [8, 2048, 4096], P(('pair', 'node'))
- s_len: int32 [8], P(('pair', 'node'))
- tokens: bfloat16 [8, 16, 4096], P(('pair', 'node'))
- c_len: int32 [8, 16], P(('pair', 'node'))
- k_cache: bfloat16 [1, 8, 16, 512, 8, 128], P(None, ('pair', 'node'), None, None, 'tp')
- v_cache: bfloat16 [1, 8, 16, 512, 8, 128], P(None, ('pair', 'node'), None, None, 'tp')
- attn_norm: bfloat16 [1, 4096], replicated
- mlp_norm: bfloat16 [1, 4096], replicated
- w_qkv_pre: bfloat16 [1, 4096, 8, 6, 128], P(None, None, 'tp')
- w_out_pre: bfloat16 [1, 8, 4, 128, 4096], P(None, 'tp')
- w_qkv_dec: bfloat16 [1, 4096, 8, 6, 128], P(None, None, 'tp')
- w_out_dec: bfloat16 [1, 8, 4, 128, 4096], P(None, 'tp')
- w_gate: bfloat16 [1, 4096, 14336], P(None, None, 'tp')
- w_up: bfloat16 [1, 4096, 14336], P(None, None, 'tp')
- w_down: bfloat16 [1, 14336, 4096], P(None, 'tp')
Outputs:
- output 1: bfloat16 [8, 2048, 4096], P(('pair', 'node'))
- output 2: bfloat16 [8, 16, 4096], P(('pair', 'node'))
- output 3: bfloat16 [1, 8, 2048, 8, 128], P(None, ('pair', 'node'), None, 'tp')
- output 4: bfloat16 [1, 8, 2048, 8, 128], P(None, ('pair', 'node'), None, 'tp')
- output 5: bfloat16 [1, 8, 16, 512, 8, 128], P(None, ('pair', 'node'), None, None, 'tp')
- output 6: bfloat16 [1, 8, 16, 512, 8, 128], P(None, ('pair', 'node'), None, None, 'tp')
All inputs are finite; a program needn't handle non-finite values.
Results may differ from a plain program's by a relative error of at most 0.00940803.
Values are sent between devices in bfloat16 or wider.
A program may use at most 768 MiB of HBM per device.

v0:
```python
import math
import jax
import jax.numpy as jnp
from jax import lax
from jax.sharding import PartitionSpec as P

NORM_EPS = 1e-5
ROPE_BASE = 10000.0
QUERY_BLOCK = 512


def rope_tables(positions, head_dim):
    inv_freq = jnp.exp(jnp.arange(head_dim // 2, dtype=jnp.float32) * (-2.0 * math.log(ROPE_BASE) / head_dim))
    angles = positions.astype(jnp.float32)[..., None] * inv_freq
    return jnp.cos(angles), jnp.sin(angles)


def apply_rope(vectors, cos_tab, sin_tab):
    half_dim = vectors.shape[-1] // 2
    vec32 = vectors.astype(jnp.float32)
    first_half = vec32[..., :half_dim]
    second_half = vec32[..., half_dim:]
    return jnp.concatenate([first_half * cos_tab - second_half * sin_tab, second_half * cos_tab + first_half * sin_tab], axis=-1).astype(jnp.bfloat16)


def rms_norm(hidden, gain_vec):
    hidden_f = hidden.astype(jnp.float32)
    inv_rms = lax.rsqrt(jnp.mean(hidden_f * hidden_f, axis=-1, keepdims=True) + NORM_EPS)
    return (hidden_f * inv_rms * gain_vec.astype(jnp.float32)).astype(jnp.bfloat16)


def residual_add(hidden, delta_bf):
    return (hidden.astype(jnp.float32) + delta_bf.astype(jnp.float32)).astype(jnp.bfloat16)


def tp_sum(partial):
    return lax.psum(partial, 'tp')


def mlp_block(hidden, gain_mlp, gate_mat, up_mat, down_mat, reduce_fn):
    normed = rms_norm(hidden, gain_mlp)
    gate_act = jnp.einsum('nse,ef->nsf', normed, gate_mat, preferred_element_type=jnp.float32).astype(jnp.bfloat16)
    up_proj = jnp.einsum('nse,ef->nsf', normed, up_mat, preferred_element_type=jnp.float32).astype(jnp.bfloat16)
    swi_act = (jax.nn.silu(gate_act.astype(jnp.float32)) * up_proj.astype(jnp.float32)).astype(jnp.bfloat16)
    down_out = reduce_fn(jnp.einsum('nsf,fe->nse', swi_act, down_mat, preferred_element_type=jnp.float32))
    return residual_add(hidden, down_out.astype(jnp.bfloat16))


def qkv_heads(hidden, gain_attn, qkv_mat, cos_tab, sin_tab):
    group_size = qkv_mat.shape[2] - 2
    normed = rms_norm(hidden, gain_attn)
    qkv_all = jnp.einsum('nse,ekcd->nskcd', normed, qkv_mat, preferred_element_type=jnp.float32).astype(jnp.bfloat16)
    q_rot = apply_rope(qkv_all[:, :, :, :group_size], cos_tab[:, :, None, None, :], sin_tab[:, :, None, None, :])
    k_rot = apply_rope(qkv_all[:, :, :, group_size], cos_tab[:, :, None, :], sin_tab[:, :, None, :])
    return q_rot, k_rot, qkv_all[:, :, :, group_size + 1]


def attn_project(context, out_mat, reduce_fn):
    return reduce_fn(jnp.einsum('nskgd,kgde->nse', context, out_mat, preferred_element_type=jnp.float32)).astype(jnp.bfloat16)


def prefill_attention(q_rot, k_rot, v_new, key_ok):
    batch_n, seq_len, kv_local, group_size, head_dim = q_rot.shape
    q_size = min(seq_len, QUERY_BLOCK)
    key_pos = jnp.arange(seq_len)
    scale_q = head_dim ** -0.5

    def attend(q_start):
        q_block = lax.dynamic_slice_in_dim(q_rot, q_start, q_size, axis=1)
        scores = jnp.einsum('nqkgd,ntkd->nkgqt', q_block, k_rot, preferred_element_type=jnp.float32) * scale_q
        q_pos = q_start + jnp.arange(q_size)
        allowed = (key_pos[None, None, :] <= q_pos[None, :, None]) & key_ok[:, None, :]
        scores = jnp.where(allowed[:, None, None], scores, -1e30)
        probs_bf = jax.nn.softmax(scores, axis=-1).astype(jnp.bfloat16)
        return jnp.einsum('nkgqt,ntkd->nqkgd', probs_bf, v_new, preferred_element_type=jnp.float32).astype(jnp.bfloat16)

    blocks = lax.map(attend, jnp.arange(seq_len // q_size) * q_size)
    return jnp.moveaxis(blocks, 0, 1).reshape(batch_n, seq_len, kv_local, group_size, head_dim)


def decode_attention(q_rot, k_rot, v_new, k_old, v_old, write_mask, seen_mask):
    k_upd = jnp.where(write_mask[:, :, :, None, None], k_rot[:, :, None], k_old)
    v_upd = jnp.where(write_mask[:, :, :, None, None], v_new[:, :, None], v_old)
    scores = jnp.einsum('nbkgd,nbtkd->nbkgt', q_rot, k_upd, preferred_element_type=jnp.float32) * (q_rot.shape[-1] ** -0.5)
    scores = jnp.where(seen_mask[:, :, None, None, :], scores, -1e30)
    probs_bf = jax.nn.softmax(scores, axis=-1).astype(jnp.bfloat16)
    context = jnp.einsum('nbkgt,nbtkd->nbkgd', probs_bf, v_upd, preferred_element_type=jnp.float32).astype(jnp.bfloat16)
    return context, k_upd, v_upd


def run_prefill(prompt, s_len, attn_norm, mlp_norm, qkv_pre, out_pre, w_gate, w_up, w_down, reduce_fn, last_mlp):
    layer_count = qkv_pre.shape[0]
    positions = jnp.arange(prompt.shape[1])
    cos_tab, sin_tab = rope_tables(positions[None, :], qkv_pre.shape[-1])
    key_ok = positions[None, :] < s_len[:, None]
    keep_mask = key_ok[:, :, None, None]
    hidden = prompt
    k_list = []
    v_list = []
    for layer_idx in range(layer_count):
        q_rot, k_rot, v_new = qkv_heads(hidden, attn_norm[layer_idx], qkv_pre[layer_idx], cos_tab, sin_tab)
        context = prefill_attention(q_rot, k_rot, v_new, key_ok)
        hidden = residual_add(hidden, attn_project(context, out_pre[layer_idx], reduce_fn))
        if last_mlp or layer_idx < layer_count - 1:
            hidden = mlp_block(hidden, mlp_norm[layer_idx], w_gate[layer_idx], w_up[layer_idx], w_down[layer_idx], reduce_fn)
        k_list.append(jnp.where(keep_mask, k_rot, jnp.zeros_like(k_rot)))
        v_list.append(jnp.where(keep_mask, v_new, jnp.zeros_like(v_new)))
    return hidden, k_list, v_list


def run_decode(tokens, c_len, k_cache, v_cache, attn_norm, mlp_norm, qkv_dec, out_dec, w_gate, w_up, w_down, reduce_fn):
    cos_tab, sin_tab = rope_tables(c_len, qkv_dec.shape[-1])
    cache_pos = jnp.arange(k_cache.shape[3])
    write_mask = cache_pos[None, None, :] == c_len[:, :, None]
    seen_mask = cache_pos[None, None, :] <= c_len[:, :, None]
    hidden = tokens
    k_list = []
    v_list = []
    for layer_idx in range(qkv_dec.shape[0]):
        q_rot, k_rot, v_new = qkv_heads(hidden, attn_norm[layer_idx], qkv_dec[layer_idx], cos_tab, sin_tab)
        context, k_upd, v_upd = decode_attention(q_rot, k_rot, v_new, k_cache[layer_idx], v_cache[layer_idx], write_mask, seen_mask)
        hidden = residual_add(hidden, attn_project(context, out_dec[layer_idx], reduce_fn))
        hidden = mlp_block(hidden, mlp_norm[layer_idx], w_gate[layer_idx], w_up[layer_idx], w_down[layer_idx], reduce_fn)
        k_list.append(k_upd)
        v_list.append(v_upd)
    return hidden, jnp.stack(k_list), jnp.stack(v_list)


def relayout_tp(kv_block, tp_count):
    batch_n, seq_len, per_dev, head_dim = kv_block.shape
    if per_dev % tp_count == 0:
        split_kv = kv_block.reshape(batch_n, seq_len, per_dev // tp_count, tp_count, head_dim)
        swapped = lax.all_to_all(split_kv, 'tp', 3, 2, tiled=True)
        return swapped.reshape(batch_n, seq_len, per_dev, head_dim)
    spread = tp_count // per_dev
    tp_index = lax.axis_index('tp')
    received = []
    for step_idx in range(per_dev):
        head_idx = (tp_index // spread + step_idx) % per_dev
        head_piece = lax.dynamic_index_in_dim(kv_block, head_idx, axis=2, keepdims=True)
        pair_list = [(src_idx, (src_idx % spread) * per_dev + (src_idx // spread + step_idx) % per_dev) for src_idx in range(tp_count)]
        received.append(lax.ppermute(head_piece, 'tp', pair_list))
    stacked = jnp.concatenate(received[::-1], axis=2)
    return jnp.roll(stacked, tp_index % per_dev + 1, axis=2)


def hand_off(kv_block, tp_count, node_count):
    node_hop = [(src_idx, (src_idx + node_count // 2) % node_count) for src_idx in range(node_count)]
    moved_kv = lax.ppermute(kv_block, 'node', node_hop)
    return relayout_tp(moved_kv, tp_count)


def solution(mesh):
    node_count = mesh.shape['node']
    tp_count = mesh.shape['tp']
    row_spec = P(('pair', 'node'), None, None)
    len_spec = P(('pair', 'node'))
    clen_spec = P(('pair', 'node'), None)
    cache_spec = P(None, ('pair', 'node'), None, None, 'tp', None)
    prompt_kv_spec = P(None, ('pair', 'node'), None, 'tp', None)
    gain_spec = P(None, None)
    qkv_spec = P(None, None, 'tp', None, None)
    out_spec = P(None, 'tp', None, None, None)
    col_spec = P(None, None, 'tp')
    down_spec = P(None, 'tp', None)

    def local_fn(prompt, s_len, tokens, c_len, k_cache, v_cache, attn_norm, mlp_norm, w_qkv_pre, w_out_pre, w_qkv_dec, w_out_dec, w_gate, w_up, w_down):
        hidden, k_list, v_list = run_prefill(prompt, s_len, attn_norm, mlp_norm, w_qkv_pre, w_out_pre, w_gate, w_up, w_down, tp_sum, True)
        k_prompt = jnp.stack([hand_off(k_block, tp_count, node_count) for k_block in k_list])
        v_prompt = jnp.stack([hand_off(v_block, tp_count, node_count) for v_block in v_list])
        tok_out, k_new, v_new = run_decode(tokens, c_len, k_cache, v_cache, attn_norm, mlp_norm, w_qkv_dec, w_out_dec, w_gate, w_up, w_down, tp_sum)
        return hidden, tok_out, k_prompt, v_prompt, k_new, v_new

    return jax.shard_map(local_fn, mesh=mesh, in_specs=(row_spec, len_spec, row_spec, clen_spec, cache_spec, cache_spec, gain_spec, gain_spec, qkv_spec, out_spec, qkv_spec, out_spec, col_spec, col_spec, down_spec), out_specs=(row_spec, row_spec, prompt_kv_spec, prompt_kv_spec, cache_spec, cache_spec), check_vma=False)
```

profile of v0, /device:TPU:104, one launch (start us, length us, event | category | flops | bytes accessed | tf_op | source)
XLA Modules:
  0.0 1852.7 jit_solution(15510954171025287201)
XLA Ops:
  1.4 30.9 %copy.35 = bf16[4096,2,6,128]{0,3,2,1:T(8,128)(2,1)} copy(bf16[4096,2,6,128]{3,1,2,0:T(2,128)(2,1)} %bitcast.221) | data formatting | bytes 25165824 | tf_op jit(solution)/shard_map/squeeze | solution.py:101
  43.0 31.6 %fusion.57 = f32[2048,1536]{0,1} fusion(bf16[4096,1536]{0,1:T(8,128)(2,1)} %bitcast.222, bf16[1,2048,4096]{2,1,0:T(8,128)(2,1)S(1)} %copy-done, f32[4096]{0:T(1024)S(1)} %bitcast.228, f32[2048]{0:T(1024)S(1)} %add_rsqrt_fusion.1), kind=kOutput, calls=%fused_computation.62 | convolution fusion | flops 25803358208 | bytes 41967616
  143.3 206.9 %while.11 = (s32[]{:T(128)}, bf16[4,1,512,2,4,128]{5,2,0,4,3,1:T(8,128)(2,1)}, s32[4]{0:T(128)S(1)}, bf16[1,2048,2,4,128]{1,4,3,2,0:T(8,128)(2,1)}, bf16[1,2048,...) while((s32[]{:T(128)}, ...), condition=%wide.region_4.5_spmd.clone, body=%wide.region_1.4_spmd.clone.sunk | while | flops 4398246400 | bytes 109142688 | solution.py:77
  148.1 16.8 fusion.186
  164.8 15.1 fusion.187
  179.9 15.2 fusion.188
  199.8 16.8 fusion.186
  216.6 15.1 fusion.187
  231.6 15.2 fusion.188
  251.5 16.8 fusion.186
  268.3 15.1 fusion.187
  283.3 15.2 fusion.188
  303.2 16.7 fusion.186
  319.9 15.1 fusion.187
  335.0 15.2 fusion.188
  350.2 24.5 %convolution_bitcast_fusion = f32[1,2048,4096]{2,1,0:T(8,128)} fusion(bf16[2048,2,4,128]{3,0,2,1:T(8,128)(2,1)} %bitcast.232, bf16[1,2,4,128,4096]{4,3,2,1,0:T(8,128)(2,1)} %param.28), kind=kOutput, calls=%fused_computation.59 | convolution fusion | flops 17179869184 | bytes 46137344 | tf_op jit(solution)/shard_map/nskgd,kgde->nse/dot_general | solution.py:59
  374.8 571.2 %all-reduce.4 = (bf16[1,2048,4096]{2,1,0:T(8,128)(2,1)}, bf16[1,16,4096]{2,1,0:T(8,128)(2,1)S(1)}) all-reduce(f32[1,2048,4096]{2,1,0:T(8,128)} %convolution_bitcast_fusion, f32[1,16,4096]{2,1,0:T(8,128)S(1)} %copy-done.11), channel_id=1, replica_groups=mesh['pair'=1,'tp'=4,'node'=8] {'tp'}, use_global_device_ids=true, to_apply=%region_5.6 | all-reduce | flops 8454144 | bytes 50724864 | tf_op jit(solution)/shard_map/psum | solution.py:37
  957.6 22.2 %fusion.79 = f32[1,16,4096]{2,1,0:T(8,128)} fusion(bf16[1,3584,4096]{2,1,0:T(8,128)(2,1)} %param.33, bf16[1,4096,3584]{2,1,0:T(8,128)(2,1)} %param.32, f32[16,3584]{1,0:T(8,128)S(1)} %fusion.85, bf16[1,16,4096]{2,1,0:T(8,128)(2,1)S(1)} %get-tuple-element.107, f32[4096]{0:T(1024)S(1)} %bitcast.225, f32[16]{0:T(128)S(1)} %add_rsqrt_fusion.2), kind=kOutput, calls=%fused_computation.78 | convolution fusion | flops 940244992 | bytes 59359296 | tf_op jit(solution)/shard_map/nsf,fe->nse/dot_general | solution.py:45
  979.8 19.9 %fusion.31 = (f32[2048]{0:T(1024)S(1)}, bf16[1,2048,4096]{2,1,0:T(8,128)(2,1)}) fusion(bf16[1,2048,4096]{2,1,0:T(8,128)(2,1)} %get-tuple-element.104, bf16[1,2048,4096]{2,1,0:T(8,128)(2,1)} %param.19), kind=kLoop, calls=%fused_computation.37 | loop fusion | flops 58718208 | bytes 50339840 | tf_op jit(solution)/shard_map/reduce_sum | solution.py:28
  999.8 73.8 %fusion.66 = bf16[2048,3584]{1,0:T(8,128)(2,1)} fusion(bf16[1,4096,3584]{2,1,0:T(8,128)(2,1)} %param.32, bf16[1,2048,4096]{2,1,0:T(8,128)(2,1)} %get-tuple-element.109, f32[4096]{0:T(1024)S(1)} %bitcast.226, f32[2048]{0:T(1024)S(1)} %add_rsqrt_fusion), kind=kOutput, calls=%fused_computation.66 | convolution fusion | flops 60170436608 | bytes 60841984 | tf_op jit(solution)/shard_map/nse,ef->nsf/dot_general | solution.py:43
  1073.6 78.6 %fusion.51 = bf16[2048,3584]{1,0:T(8,128)(2,1)} fusion(bf16[2048,3584]{1,0:T(8,128)(2,1)} %fusion.66, bf16[1,4096,3584]{2,1,0:T(8,128)(2,1)} %param.31, bf16[1,2048,4096]{2,1,0:T(8,128)(2,1)} %get-tuple-element.109, f32[4096]{0:T(1024)S(1)} %bitcast.227, f32[2048]{0:T(1024)S(1)} %add_rsqrt_fusion), kind=kOutput, calls=%fused_computation.57 | convolution fusion | flops 60229156864 | bytes 75522048 | tf_op jit(solution)/shard_map/nse,ef->nsf/dot_general | solution.py:42
  1152.2 72.8 %fusion.52 = f32[1,2048,4096]{2,1,0:T(8,128)} fusion(bf16[2048,3584]{1,0:T(8,128)(2,1)} %fusion.51, bf16[1,3584,4096]{2,1,0:T(8,128)(2,1)} %param.33), kind=kOutput, calls=%fused_computation.58 | convolution fusion | flops 60129542144 | bytes 77594624 | tf_op jit(solution)/shard_map/nsf,fe->nse/dot_general | solution.py:45
  1225.0 564.2 %all-reduce.5 = (bf16[1,2048,4096]{2,1,0:T(8,128)(2,1)}, bf16[1,16,4096]{2,1,0:T(8,128)(2,1)S(1)}) all-reduce(f32[1,2048,4096]{2,1,0:T(8,128)} %fusion.52, f32[1,16,4096]{2,1,0:T(8,128)S(1)} %copy-done.10), channel_id=1, replica_groups=mesh['pair'=1,'tp'=4,'node'=8] {'tp'}, use_global_device_ids=true, to_apply=%region_7.8 | all-reduce | flops 8454144 | bytes 50724864 | tf_op jit(solution)/shard_map/psum | solution.py:37
  1789.2 20.6 %fusion.34 = bf16[1,2048,4096]{2,1,0:T(8,128)(2,1)} fusion(bf16[1,2048,4096]{2,1,0:T(8,128)(2,1)} %get-tuple-element.109, bf16[1,2048,4096]{2,1,0:T(8,128)(2,1)} %get-tuple-element.102), kind=kLoop, calls=%fused_computation.40 | loop fusion | flops 33554432 | bytes 50331648 | tf_op jit(solution)/shard_map/convert_element_type | solution.py:33
  (121 shorter events, 144.0 us)
Async XLA Ops:
  74.5 15.9 copy-start.12
  85.0 18.4 copy-start.21
  86.9 1735.7 %collective-permute-start = (bf16[1,2048,2,128]{1,3,2,0:T(8,128)(2,1)}, bf16[1,2048,2,128]{1,3,2,0:T(8,128)(2,1)}, u32[]{:S(2)}, u32[]{:S(2)}) collective-permute-start(bf16[1,2048,2,128]{1,3,2,0:T(8,128)(2,1)} %get-tuple-element.122), channel_id=1, source_target_pairs={{0,4},{1,5},{2,6},{3,7},{4,0},{5,1},{6,2},{7,3},{8,12},{9,13},{10,... | collective-permute-start | bytes 3145736 | tf_op jit(solution)/shard_map/ppermute | solution.py:149
  90.2 1741.1 %collective-permute-start.3 = (bf16[1,2048,2,128]{1,3,2,0:T(8,128)(2,1)}, bf16[1,2048,2,128]{1,3,2,0:T(8,128)(2,1)}, u32[]{:S(2)}, u32[]{:S(2)}) collective-permute-start(bf16[1,2048,2,128]{1,3,2,0:T(8,128)(2,1)} %get-tuple-element.136), channel_id=1, source_target_pairs={{0,4},{1,5},{2,6},{3,7},{4,0},{5,1},{6,2},{7,3},{8,12},{9,13},{10,... | collective-permute-start | bytes 3145736 | tf_op jit(solution)/shard_map/ppermute | solution.py:149
  103.7 26.3 %copy-start.14 = (bf16[16,2,128]{2,1,0:T(2,128)(2,1)}, bf16[16,2,128]{2,1,0:T(2,128)(2,1)S(1)}, u32[]{:S(2)}) copy-start(bf16[16,2,128]{2,1,0:T(2,128)(2,1)S(1)} %copy.44) | copy-start | bytes 24580
  103.7 26.2 %copy-start.16 = (bf16[16,2,128]{2,1,0:T(2,128)(2,1)}, bf16[16,2,128]{2,1,0:T(2,128)(2,1)S(1)}, u32[]{:S(2)}) copy-start(bf16[16,2,128]{2,1,0:T(2,128)(2,1)S(1)} %copy.47) | copy-start | bytes 24580
  103.8 26.2 %copy-start.18 = (pred[16,512]{1,0:T(8,128)(4,1)}, pred[16,512]{1,0:T(8,128)(4,1)S(1)}, u32[]{:S(2)}) copy-start(pred[16,512]{1,0:T(8,128)(4,1)S(1)} %get-tuple-element.140) | copy-start | bytes 24580
  104.0 26.0 %copy-start.7 = (bf16[1,2048,2,128]{1,3,2,0:T(8,128)(2,1)S(1)}, bf16[1,2048,2,128]{1,3,2,0:T(8,128)(2,1)}, u32[]{:S(2)}) copy-start(bf16[1,2048,2,128]{1,3,2,0:T(8,128)(2,1)} %get-tuple-element.123) | copy-start | bytes 3145732
  118.1 13.2 copy-start.4
  118.1 13.2 copy-start.6
  350.2 24.5 %copy-start.11 = (f32[1,16,4096]{2,1,0:T(8,128)S(1)}, f32[1,16,4096]{2,1,0:T(8,128)}, u32[]{:S(2)}) copy-start(f32[1,16,4096]{2,1,0:T(8,128)} %fusion.76) | copy-start | bytes 786436
  374.7 571.3 %copy-start.13 = (bf16[1,16,4096]{2,1,0:T(8,128)(2,1)S(1)}, bf16[1,16,4096]{2,1,0:T(8,128)(2,1)}, u32[]{:S(2)}) copy-start(bf16[1,16,4096]{2,1,0:T(8,128)(2,1)} %param.21) | copy-start | bytes 393220
  374.8 571.4 %copy-start.20 = (bf16[1,4096]{1,0:T(2,128)(2,1)S(1)}, bf16[1,4096]{1,0:T(2,128)(2,1)}, u32[]{:S(2)}) copy-start(bf16[1,4096]{1,0:T(2,128)(2,1)} %param.26) | copy-start | bytes 24580
  1152.2 72.8 %copy-start.10 = (f32[1,16,4096]{2,1,0:T(8,128)S(1)}, f32[1,16,4096]{2,1,0:T(8,128)}, u32[]{:S(2)}) copy-start(f32[1,16,4096]{2,1,0:T(8,128)} %fusion.79) | copy-start | bytes 786436
  1789.2 20.6 %copy-start.1 = (bf16[1,1,16,512,2,128]{5,4,3,2,1,0:T(2,128)(2,1)S(1)}, bf16[1,1,16,512,2,128]{5,4,3,2,1,0:T(2,128)(2,1)}, u32[]{:S(2)}) copy-start(bf16[1,1,16,512,2,128]{5,4,3,2,1,0:T(2,128)(2,1)} %param.23) | copy-start | bytes 12582916
  1789.2 20.6 %copy-start.2 = (bf16[1,1,16,512,2,128]{5,4,3,2,1,0:T(2,128)(2,1)S(1)}, bf16[1,1,16,512,2,128]{5,4,3,2,1,0:T(2,128)(2,1)}, u32[]{:S(2)}) copy-start(bf16[1,1,16,512,2,128]{5,4,3,2,1,0:T(2,128)(2,1)} %param.24) | copy-start | bytes 12582916
  1789.2 20.6 %copy-start.15 = (bf16[16,2,128]{2,1,0:T(2,128)(2,1)S(1)}, bf16[16,2,128]{2,1,0:T(2,128)(2,1)}, u32[]{:S(2)}) copy-start(bf16[16,2,128]{2,1,0:T(2,128)(2,1)} %copy-done.14) | copy-start | bytes 24580
  1789.2 20.6 %copy-start.17 = (bf16[16,2,128]{2,1,0:T(2,128)(2,1)S(1)}, bf16[16,2,128]{2,1,0:T(2,128)(2,1)}, u32[]{:S(2)}) copy-start(bf16[16,2,128]{2,1,0:T(2,128)(2,1)} %copy-done.16) | copy-start | bytes 24580
  1789.2 20.6 %copy-start.19 = (pred[16,512]{1,0:T(8,128)(4,1)S(1)}, pred[16,512]{1,0:T(8,128)(4,1)}, u32[]{:S(2)}) copy-start(pred[16,512]{1,0:T(8,128)(4,1)} %copy-done.18) | copy-start | bytes 24580
  1809.8 25.7 %copy-start.9 = (bf16[1,16,4096]{2,1,0:T(8,128)(2,1)S(1)}, bf16[1,16,4096]{2,1,0:T(8,128)(2,1)}, u32[]{:S(2)}) copy-start(bf16[1,16,4096]{2,1,0:T(8,128)(2,1)} %copy-done.8) | copy-start | bytes 393220
  1824.6 14.9 collective-permute-start.1
  1826.8 17.1 collective-permute-start.2
  1833.6 13.1 collective-permute-start.4
  1833.6 16.0 collective-permute-start.5
  (4 other events, 23.9 us)
where the time goes:
time: 1860 us; the launch traced here: 1850 us
  blocking collectives  1140 us (61%)
  matrix products  463 us (25%)
  other arithmetic  173 us (9%)
  local copies, waits for them, and re-layouts  48.4 us (3%)
    psum x2, blocking collectives, tp_sum(): return lax.psum(partial, 'tp')  1140 us
    dot_general x2, matrix products, mlp_block(): jnp.einsum('nsf,fe->nse', swi_act, down_mat, preferred_element_type=jnp.f...  95.1 us
    dot_general x2, matrix products, mlp_block(): jnp.einsum('nse,ef->nsf', normed, gate_mat, preferred_element_type=jnp.fl...  90 us
    dot_general x1, matrix products, mlp_block(): jnp.einsum('nse,ef->nsf', normed, up_mat, preferred_element_type=jnp.floa...  73.8 us
    dot_general x4, matrix products, attend(): jnp.einsum('nqkgd,ntkd->nkgqt', q_block, k_rot, preferred_element_type=jn...  67.1 us
    dot_general x4, matrix products, attend(): jnp.einsum('nkgqt,ntkd->nqkgd', probs_bf, v_new, preferred_element_type=j...  61 us
    reduce_sum x4, other arithmetic, attend(): probs_bf = jax.nn.softmax(scores, axis=-1).astype(jnp.bfloat16)  60.2 us
  transfers between devices with their start and end apart: 6, of which 3 were waited for; matrix products, arithmetic and copies ran while one was open for 32% of the time, Pallas kernels for 0%

commit v1 on v0

v1 whole, which is shorter than its diff:
```python
import functools
import math
import jax
import jax.numpy as jnp
from jax import lax
from jax.experimental import pallas as pl
from jax.experimental.pallas import tpu as pltpu
from jax.sharding import PartitionSpec as P

NORM_EPS = 1e-5
ROPE_BASE = 10000.0
CHUNKS = 4
F32 = jnp.float32
BF16 = jnp.bfloat16


def rope_tables(positions, head_dim):
    inv_freq = jnp.exp(jnp.arange(head_dim // 2, dtype=F32) * (-2.0 * math.log(ROPE_BASE) / head_dim))
    angles = positions.astype(F32)[..., None] * inv_freq
    return jnp.cos(angles), jnp.sin(angles)


def apply_rope(vectors, cos_tab, sin_tab):
    half_dim = vectors.shape[-1] // 2
    vec32 = vectors.astype(F32)
    first_half = vec32[..., :half_dim]
    second_half = vec32[..., half_dim:]
    return jnp.concatenate([first_half * cos_tab - second_half * sin_tab, second_half * cos_tab + first_half * sin_tab], axis=-1).astype(BF16)


def rms_norm(hidden, gain_vec):
    hidden_f = hidden.astype(F32)
    inv_rms = lax.rsqrt(jnp.mean(hidden_f * hidden_f, axis=-1, keepdims=True) + NORM_EPS)
    return (hidden_f * inv_rms * gain_vec.astype(F32)).astype(BF16)


def residual_add(hidden, delta_bf):
    return (hidden.astype(F32) + delta_bf.astype(F32)).astype(BF16)


def dot32(a, b):
    return jnp.dot(a, b, preferred_element_type=F32)


def kv_prep_kernel(slen_ref, *refs, kv_local, head_dim, rows):
    k_refs = refs[:kv_local]
    v_refs = refs[kv_local:2 * kv_local]
    cos_ref, sin_ref, k_out, pack_out = refs[2 * kv_local:]
    pos = pl.program_id(0) * rows + lax.broadcasted_iota(jnp.int32, (rows, head_dim), 0)
    keep = pos < slen_ref[0]
    for head in range(kv_local):
        k32 = k_refs[head][...].astype(F32)
        k_rot = (k32 * cos_ref[...] + pltpu.roll(k32, head_dim // 2, 1) * sin_ref[...]).astype(BF16)
        k_out[:, head * head_dim:(head + 1) * head_dim] = k_rot
        zero = jnp.zeros_like(k_rot)
        pack_out[head, 0] = jnp.where(keep, k_rot, zero)
        pack_out[head, 1] = jnp.where(keep, v_refs[head][...], zero)


def kv_prep(qkv, s_len, cos_full, sin_full, kv_local, group_size, head_dim):
    seq_len = qkv.shape[0]
    rows = 512
    per_kv = group_size + 2
    col = lambda c: pl.BlockSpec((rows, head_dim), lambda r, c=c: (r, c))
    in_specs = [pl.BlockSpec(memory_space=pltpu.SMEM)]
    in_specs += [col(h * per_kv + group_size) for h in range(kv_local)]
    in_specs += [col(h * per_kv + group_size + 1) for h in range(kv_local)]
    in_specs += [col(0), col(0)]
    return pl.pallas_call(
        functools.partial(kv_prep_kernel, kv_local=kv_local, head_dim=head_dim, rows=rows),
        grid=(seq_len // rows,),
        in_specs=in_specs,
        out_specs=[pl.BlockSpec((rows, kv_local * head_dim), lambda r: (r, 0)), pl.BlockSpec((kv_local, 2, rows, head_dim), lambda r: (0, 0, r, 0))],
        out_shape=[jax.ShapeDtypeStruct((seq_len, kv_local * head_dim), BF16), jax.ShapeDtypeStruct((kv_local, 2, seq_len, head_dim), BF16)],
        cost_estimate=pl.CostEstimate(flops=seq_len * 4096, bytes_accessed=seq_len * 3072, transcendentals=0),
        name="kv_prep",
    )(s_len, *([qkv] * (2 * kv_local)), cos_full, sin_full)


def attend_kernel(slen_ref, q_ref, cos_ref, sin_ref, k_ref, v_ref, out_ref, *, start, rows, sub):
    head_dim = q_ref.shape[1]
    scale = (head_dim ** -0.5) * math.log2(math.e)
    q32 = q_ref[...].astype(F32)
    q_rot = (q32 * cos_ref[...] + pltpu.roll(q32, head_dim // 2, 1) * sin_ref[...]).astype(BF16)
    dims = (((1,), (1,)), ((), ()))
    for part in range(rows // sub):
        q_part = q_rot[part * sub:(part + 1) * sub]
        base = start + part * sub
        width = base + sub
        tail = lax.dot_general(q_part, k_ref[base:width], dims, preferred_element_type=F32)
        q_pos = lax.broadcasted_iota(jnp.int32, (sub, sub), 0)
        k_pos = lax.broadcasted_iota(jnp.int32, (sub, sub), 1)
        allowed = (k_pos <= q_pos) & (k_pos + base < slen_ref[0])
        tail = jnp.where(allowed, tail, -1e30)
        top = jnp.max(tail, axis=1, keepdims=True)
        if base > 0:
            body = lax.dot_general(q_part, k_ref[:base], dims, preferred_element_type=F32)
            safe = 1536
            if base > safe:
                k_head = lax.broadcasted_iota(jnp.int32, (sub, base - safe), 1) + safe
                late = jnp.where(k_head < slen_ref[0], body[:, safe:], -1e30)
                body = jnp.concatenate([body[:, :safe], late], axis=1)
            top = jnp.maximum(top, jnp.max(body, axis=1, keepdims=True))
            p_body = jnp.exp2((body - top) * scale)
            p_tail = jnp.exp2((tail - top) * scale)
            inv = 1.0 / (jnp.sum(p_body, axis=1, keepdims=True) + jnp.sum(p_tail, axis=1, keepdims=True))
            acc = dot32((p_body * inv).astype(BF16), v_ref[:base]) + dot32((p_tail * inv).astype(BF16), v_ref[base:width])
        else:
            p_tail = jnp.exp2((tail - top) * scale)
            inv = 1.0 / jnp.sum(p_tail, axis=1, keepdims=True)
            acc = dot32((p_tail * inv).astype(BF16), v_ref[base:width])
        out_ref[part * sub:(part + 1) * sub, :] = acc.astype(BF16)


def attend_chunk(qkv, k_rot, cos_full, sin_full, s_len, chunk, rows, kv_local, group_size, head_dim):
    heads = kv_local * group_size
    per_kv = group_size + 2
    width = (chunk + 1) * rows
    tab = pl.BlockSpec((rows, head_dim), lambda h: (chunk, 0))
    return pl.pallas_call(
        functools.partial(attend_kernel, start=chunk * rows, rows=rows, sub=256),
        grid=(heads,),
        in_specs=[
            pl.BlockSpec(memory_space=pltpu.SMEM),
            pl.BlockSpec((rows, head_dim), lambda h: (chunk, (h // group_size) * per_kv + h % group_size)),
            tab,
            tab,
            pl.BlockSpec((width, head_dim), lambda h: (0, h // group_size)),
            pl.BlockSpec((width, head_dim), lambda h: (0, (h // group_size) * per_kv + group_size + 1)),
        ],
        out_specs=pl.BlockSpec((rows, head_dim), lambda h: (0, h)),
        out_shape=jax.ShapeDtypeStruct((rows, heads * head_dim), BF16),
        cost_estimate=pl.CostEstimate(flops=4 * rows * width * heads * head_dim * 3, bytes_accessed=4 * rows * heads * head_dim, transcendentals=rows * width * heads),
        name="attend",
    )(s_len, qkv, cos_full, sin_full, k_rot, qkv)


def project_kernel(place_ref, *refs, tp_count, n_in):
    ctx_refs = refs[:n_in]
    w_ref, x_ref, h_ref, ctx_all = refs[n_in:]

    @pl.when(pl.program_id(0) == 0)
    def _():
        if n_in == 1:
            ctx_all[...] = ctx_refs[0][...]
        else:
            own, succ, far_a, far_b, prev = ctx_refs
            me = place_ref[0]
            half = far_a.shape[0]
            ctx_all[me] = own[...]
            ctx_all[lax.rem(me + 1, tp_count)] = succ[...]
            ctx_all[lax.rem(me + 2, tp_count), :half] = far_a[...]
            ctx_all[lax.rem(me + 2, tp_count), half:] = far_b[...]
            ctx_all[lax.rem(me + 3, tp_count)] = prev[...]

    depth = ctx_all.shape[2]
    acc = dot32(ctx_all[0], w_ref[:depth])
    for block in range(1, tp_count):
        acc += dot32(ctx_all[block], w_ref[block * depth:(block + 1) * depth])
    h_ref[...] = (x_ref[...].astype(F32) + acc.astype(BF16).astype(F32)).astype(BF16)


def project_chunk(ctx_parts, out_full, x, row_block, rows, place, tp_count, tile=512):
    full_depth, width = out_full.shape
    depth = full_depth // tp_count
    whole = lambda part: pl.BlockSpec(part.shape, lambda j: (0,) * part.ndim, pipeline_mode=pl.Buffered(1))
    return pl.pallas_call(
        functools.partial(project_kernel, tp_count=tp_count, n_in=len(ctx_parts)),
        grid=(width // tile,),
        in_specs=[pl.BlockSpec(memory_space=pltpu.SMEM)] + [whole(p) for p in ctx_parts] + [
            pl.BlockSpec((full_depth, tile), lambda j: (0, j)),
            pl.BlockSpec((rows, tile), lambda j: (row_block, j)),
        ],
        out_specs=pl.BlockSpec((rows, tile), lambda j: (0, j)),
        out_shape=jax.ShapeDtypeStruct((rows, width), BF16),
        scratch_shapes=[pltpu.VMEM((tp_count, rows, depth), BF16)],
        compiler_params=pltpu.CompilerParams(vmem_limit_bytes=40 * 1024 * 1024),
        cost_estimate=pl.CostEstimate(flops=2 * rows * full_depth * width, bytes_accessed=2 * full_depth * width, transcendentals=0),
        name="project",
    )(place, *ctx_parts, out_full, x)


def mlp_kernel(h_ref, gain_ref, wg_ref, wu_ref, wd_ref, out_ref, m_ref):
    step = pl.program_id(0)
    rows, _ = h_ref.shape
    sub = min(rows, 128)

    @pl.when(step == 0)
    def _():
        @pl.loop(0, rows // sub)
        def _(part):
            at = pl.ds(pl.multiple_of(part * sub, sub), sub)
            h32 = h_ref[at, :].astype(F32)
            inv_rms = lax.rsqrt(jnp.mean(h32 * h32, axis=-1, keepdims=True) + NORM_EPS)
            m_ref[at, :] = (h32 * inv_rms * gain_ref[...].astype(F32)).astype(BF16)

    gate_act = dot32(m_ref[...], wg_ref[...]).astype(BF16).astype(F32)
    up_proj = dot32(m_ref[...], wu_ref[...]).astype(BF16).astype(F32)
    swi_act = (jax.nn.silu(gate_act) * up_proj).astype(BF16)

    @pl.when(step == 0)
    def _():
        out_ref[...] = dot32(swi_act, wd_ref[...])

    @pl.when(step > 0)
    def _():
        out_ref[...] += dot32(swi_act, wd_ref[...])


def mlp_chunk(hidden, gain, gate_mat, up_mat, down_mat, tile=512):
    rows, width = hidden.shape
    ff = gate_mat.shape[1]
    once = lambda shape: pl.BlockSpec(shape, lambda f: (0, 0), pipeline_mode=pl.Buffered(1))
    return pl.pallas_call(
        mlp_kernel,
        grid=(ff // tile,),
        in_specs=[
            once((rows, width)),
            once((1, width)),
            pl.BlockSpec((width, tile), lambda f: (0, f)),
            pl.BlockSpec((width, tile), lambda f: (0, f)),
            pl.BlockSpec((tile, width), lambda f: (f, 0)),
        ],
        out_specs=pl.BlockSpec((rows, width), lambda f: (0, 0), pipeline_mode=pl.Buffered(1)),
        out_shape=jax.ShapeDtypeStruct((rows, width), F32),
        scratch_shapes=[pltpu.VMEM((rows, width), BF16)],
        compiler_params=pltpu.CompilerParams(vmem_limit_bytes=60 * 1024 * 1024),
        cost_estimate=pl.CostEstimate(flops=6 * rows * width * ff, bytes_accessed=6 * width * ff, transcendentals=rows * ff),
        name="mlp",
    )(hidden, gain, gate_mat, up_mat, down_mat)


def after(value, *deps):
    return lax.optimization_barrier((value,) + deps)[0]


def make_ring(tp_count):
    up = [(i, (i + 1) % tp_count) for i in range(tp_count)]
    down = [((i + 1) % tp_count, i) for i in range(tp_count)]
    return (lambda x: lax.ppermute(x, 'tp', up)), (lambda x: lax.ppermute(x, 'tp', down))


def ring_gather(block, tp_count):
    send_up, send_down = make_ring(tp_count)
    half = block.shape[0] // 2
    prev = send_up(block)
    succ = send_down(block)
    return [block, succ, send_up(prev[:half]), send_down(succ[half:]), prev]


def scatter_first(partial, tp_count, me):
    send_up, send_down = make_ring(tp_count)
    half = partial.shape[1] // 2
    far_at = (me + 2) % tp_count
    width = partial.shape[2]
    lower = lax.dynamic_slice(partial, (far_at, 0, 0), (1, half, width))[0]
    upper = lax.dynamic_slice(partial, (far_at, half, 0), (1, half, width))[0]
    from_prev = send_up(lower)
    from_succ = send_down(upper)
    return from_prev, from_succ


def scatter_add(partial, first, tp_count, me):
    from_prev, from_succ = first
    half = partial.shape[1] // 2
    pick = lambda dist: lax.dynamic_index_in_dim(partial, (me + dist) % tp_count, axis=0, keepdims=False)
    succ, prev = pick(1), pick(3)
    up_block = jnp.concatenate([succ[:half] + from_prev, succ[half:]], axis=0)
    down_block = jnp.concatenate([prev[:half], prev[half:] + from_succ], axis=0)
    return up_block, down_block


def scatter_last(partial, blocks, tp_count, me):
    send_up, send_down = make_ring(tp_count)
    own = lax.dynamic_index_in_dim(partial, me, axis=0, keepdims=False)
    from_prev = send_up(blocks[0])
    from_succ = send_down(blocks[1])
    return own + (from_prev + from_succ)


def small_sum(partial, tp_count):
    send_up, send_down = make_ring(tp_count)
    far = lax.ppermute(partial, 'tp', [(i, (i + 2) % tp_count) for i in range(tp_count)])
    return (partial + far) + (send_up(partial) + send_down(partial))


def hand_off(pack, tp_count, node_count, tp_index):
    kv_local = pack.shape[0]
    spread = tp_count // kv_local
    got = []
    for step in range(kv_local):
        head = (tp_index // spread + step) % kv_local
        piece = lax.dynamic_index_in_dim(pack, head, axis=0, keepdims=False)
        pairs = []
        for node in range(node_count):
            for src in range(tp_count):
                h = (src // spread + step) % kv_local
                dst = (src % spread) * kv_local + h
                pairs.append((src * node_count + node, dst * node_count + (node + node_count // 2) % node_count))
        got.append(lax.ppermute(piece, ('tp', 'node'), pairs))
    first = jnp.stack([got[0], got[1]], axis=2)
    second = jnp.stack([got[1], got[0]], axis=2)
    both = jnp.where(tp_index % kv_local == 0, first, second)
    return both[0][None, None], both[1][None, None]


def decode_attention(q_rot, k_rot, v_new, k_old, v_old, write_mask, seen_mask):
    k_upd = jnp.where(write_mask[:, :, :, None, None], k_rot[:, :, None], k_old)
    v_upd = jnp.where(write_mask[:, :, :, None, None], v_new[:, :, None], v_old)
    scores = jnp.einsum('nbkgd,nbtkd->nbkgt', q_rot, k_upd, preferred_element_type=F32) * (q_rot.shape[-1] ** -0.5)
    scores = jnp.where(seen_mask[:, :, None, None, :], scores, -1e30)
    probs_bf = jax.nn.softmax(scores, axis=-1).astype(BF16)
    context = jnp.einsum('nbkgt,nbtkd->nbkgd', probs_bf, v_upd, preferred_element_type=F32).astype(BF16)
    return context, k_upd, v_upd


def mlp_partial(hidden, gain, gate_mat, up_mat, down_mat):
    normed = rms_norm(hidden, gain)
    gate_act = dot32(normed, gate_mat).astype(BF16)
    up_proj = dot32(normed, up_mat).astype(BF16)
    swi_act = (jax.nn.silu(gate_act.astype(F32)) * up_proj.astype(F32)).astype(BF16)
    return dot32(swi_act, down_mat)


def run_decode(tokens, hold, c_len, k_cache, v_cache, attn_gain, mlp_gain, qkv_dec, out_dec, gate_mat, up_mat, down_mat, tp_count):
    group_size = qkv_dec.shape[2] - 2
    cos_tab, sin_tab = rope_tables(c_len, qkv_dec.shape[-1])
    cache_pos = jnp.arange(k_cache.shape[2])
    write_mask = cache_pos[None, None, :] == c_len[:, :, None]
    seen_mask = cache_pos[None, None, :] <= c_len[:, :, None]
    normed = rms_norm(tokens, attn_gain)
    qkv_all = jnp.einsum('nse,ekcd->nskcd', normed, qkv_dec, preferred_element_type=F32).astype(BF16)
    q_rot = apply_rope(qkv_all[:, :, :, :group_size], cos_tab[:, :, None, None, :], sin_tab[:, :, None, None, :])
    k_rot = apply_rope(qkv_all[:, :, :, group_size], cos_tab[:, :, None, :], sin_tab[:, :, None, :])
    context, k_upd, v_upd = decode_attention(q_rot, k_rot, qkv_all[:, :, :, group_size + 1], k_cache, v_cache, write_mask, seen_mask)
    attn_part = jnp.einsum('nskgd,kgde->nse', context, out_dec, preferred_element_type=F32)
    hidden = residual_add(tokens, small_sum(attn_part, tp_count).astype(BF16))
    hidden = after(hidden, hold)
    down_part = mlp_partial(hidden[0], mlp_gain, gate_mat, up_mat, down_mat)[None]
    hidden = residual_add(hidden, small_sum(down_part, tp_count).astype(BF16))
    return hidden, k_upd[None], v_upd[None]


def solution(mesh):
    node_count = mesh.shape['node']
    tp_count = mesh.shape['tp']
    row_spec = P(('pair', 'node'), None, None)
    len_spec = P(('pair', 'node'))
    clen_spec = P(('pair', 'node'), None)
    cache_spec = P(None, ('pair', 'node'), None, None, 'tp', None)
    prompt_kv_spec = P(None, ('pair', 'node'), None, 'tp', None)
    gain_spec = P(None, None)
    qkv_spec = P(None, None, 'tp', None, None)
    out_spec = P(None, 'tp', None, None, None)
    col_spec = P(None, None, 'tp')
    down_spec = P(None, 'tp', None)

    def local_fn(prompt, s_len, tokens, c_len, k_cache, v_cache, attn_norm, mlp_norm, w_qkv_pre, w_out_pre, w_qkv_dec, w_out_dec, w_gate, w_up, w_down):
        tp_index = lax.axis_index('tp')
        node_index = lax.axis_index('node')
        width = prompt.shape[-1]
        seq_len = prompt.shape[1]
        kv_local, per_kv, head_dim = w_qkv_pre.shape[2:]
        group_size = per_kv - 2
        gate_mat, up_mat, down_mat = w_gate[0], w_up[0], w_down[0]

        out_local = w_out_pre[0].reshape(kv_local * group_size * head_dim, width)
        slice_rows = out_local.shape[0] // node_count
        out_slice = lax.dynamic_slice_in_dim(out_local, node_index * slice_rows, slice_rows, axis=0)
        out_full = lax.all_gather(out_slice, ('tp', 'node'), axis=0, tiled=True)

        x = prompt[0]
        qkv = dot32(rms_norm(x, attn_norm[0]), w_qkv_pre[0].reshape(width, kv_local * per_kv * head_dim)).astype(BF16)
        cos_tab, sin_tab = rope_tables(jnp.arange(seq_len), head_dim)
        cos_full = jnp.concatenate([cos_tab, cos_tab], axis=-1)
        sin_full = jnp.concatenate([-sin_tab, sin_tab], axis=-1)
        k_rot, pack = kv_prep(qkv, s_len, cos_full, sin_full, kv_local, group_size, head_dim)

        rows = seq_len // CHUNKS
        own_rows = rows // tp_count
        place = tp_index.astype(jnp.int32)[None]
        contexts = [attend_chunk(qkv, k_rot, cos_full, sin_full, s_len, c, rows, kv_local, group_size, head_dim) for c in range(CHUNKS)]
        ctx_parts = [ring_gather(contexts[0], tp_count)]
        ctx_parts += [[lax.all_gather(context, 'tp', axis=0)] for context in contexts[1:]]
        partials, blocks, finals, hiddens, firsts = [], [], [], [], []

        def finish(c):
            summed = scatter_last(partials[c], blocks[c], tp_count, tp_index)
            own_hidden = lax.dynamic_slice_in_dim(hiddens[c], tp_index * own_rows, own_rows, axis=0)
            finals.append(residual_add(own_hidden, summed.astype(BF16)))

        for chunk in range(CHUNKS):
            deps = []
            if chunk >= 2:
                finish(chunk - 2)
                deps.append(finals[chunk - 2])
            if chunk >= 1:
                deps.append(partials[chunk - 1])
            parts = ctx_parts[chunk]
            if deps:
                parts = list(lax.optimization_barrier(tuple(parts) + tuple(deps))[:len(parts)])
            hidden = project_chunk(parts, out_full, x, chunk, rows, place, tp_count)
            if chunk >= 1:
                blocks.append(scatter_add(partials[chunk - 1], firsts[chunk - 1], tp_count, tp_index))
                hidden = after(hidden, *blocks[chunk - 1])
            hiddens.append(hidden)
            partial = mlp_chunk(hidden, mlp_norm, gate_mat, up_mat, down_mat).reshape(tp_count, own_rows, width)
            partials.append(partial)
            firsts.append(scatter_first(partial, tp_count, tp_index))
        finish(CHUNKS - 2)
        blocks.append(scatter_add(partials[-1], firsts[-1], tp_count, tp_index))
        finish(CHUNKS - 1)
        out = jnp.concatenate([lax.all_gather(final, 'tp', axis=0, tiled=True) for final in finals], axis=0)

        k_prompt, v_prompt = hand_off(pack, tp_count, node_count, tp_index)
        tok_out, k_new, v_new = run_decode(after(tokens, partials[CHUNKS - 1]), partials[CHUNKS - 1], c_len, k_cache[0], v_cache[0], attn_norm[0], mlp_norm[0], w_qkv_dec[0], w_out_dec[0], gate_mat, up_mat, down_mat, tp_count)
        return out[None], tok_out, k_prompt, v_prompt, k_new, v_new

    return jax.shard_map(local_fn, mesh=mesh, in_specs=(row_spec, len_spec, row_spec, clen_spec, cache_spec, cache_spec, gain_spec, gain_spec, qkv_spec, out_spec, qkv_spec, out_spec, col_spec, col_spec, down_spec), out_specs=(row_spec, row_spec, prompt_kv_spec, prompt_kv_spec, cache_spec, cache_spec), check_vma=False)
```

time: 1860 us -> 929 us (0.50)
  blocking collectives: 1140 us -> 0 us
  Pallas kernels: 0 us -> 398 us
  matrix products: 463 us -> 85.4 us
  waiting for transfers between devices: 10.5 us -> 199 us
  other arithmetic: 173 us -> 95.6 us
  starting transfers between devices: 12.1 us -> 45.4 us
  local copies, waits for them, and re-layouts: 48.4 us -> 77.5 us
    psum x2 -> x0, blocking collectives: 1140 us -> none  [tp_sum(): return lax.psum(partial, 'tp')]
    pallas_call x0 -> x13, Pallas kernels: none -> 398 us  [the longest x4 245 us: mlp_chunk(): pl.pallas_call(mlp_kernel, grid=(ff // tile,), in_specs=[once((rows, widt...]
    dot_general x16 -> x5, matrix products: 425 us -> 78.1 us  [the longest x3 68.8 us: dot32(): return jnp.dot(a, b, preferred_element_type=F32)]
    ppermute x6 -> x28, waiting for transfers between devices: 10.5 us -> 196 us  [the longest x12 100 us: make_ring(): lax.ppermute(x, 'tp', down)]
    reduce_sum x4 -> x0, other arithmetic: 60.2 us -> none  [attend(): probs_bf = jax.nn.softmax(scores, axis=-1).astype(jnp.bfloat16)]
    unnamed x48 -> x53, local copies, waits for them, and re-layouts: 10.8 us -> 58.5 us
    ppermute x6 -> x28, starting transfers between devices: 12.1 us -> 44.1 us  [the longest x12 17 us: make_ring(): lax.ppermute(x, 'tp', up)]
    unnamed x1 -> x0, matrix products: 31.6 us -> none
  transfers between devices with their start and end apart: 6 -> 36, of which waited for: 3 -> 11; matrix products, arithmetic and copies ran while one was open for 32% -> 26% of each run, Pallas kernels for 0% -> 43%
where the time goes in v1:
time: 929 us; the launch traced here: 917 us
  Pallas kernels  398 us (43%)
  waiting for transfers between devices  199 us (21%)
  other arithmetic  95.6 us (10%)
  matrix products  85.4 us (9%)
  local copies, waits for them, and re-layouts  77.5 us (8%)
  starting transfers between devices  45.4 us (5%)
  between operations  15.8 us (2%)
    pallas_call x4, Pallas kernels, mlp_chunk(): pl.pallas_call(mlp_kernel, grid=(ff // tile,), in_specs=[once((rows, widt...  245 us
    ppermute x12, waiting for transfers between devices, make_ring(): lax.ppermute(x, 'tp', down)  100 us
    ppermute x12, waiting for transfers between devices, make_ring(): lax.ppermute(x, 'tp', up)  87.5 us
    pallas_call x4, Pallas kernels, project_chunk(): pl.pallas_call(functools.partial(project_kernel, tp_count=tp_count, n_in=...  87.4 us
    dot_general x3, matrix products, dot32(): return jnp.dot(a, b, preferred_element_type=F32)  68.8 us
    pallas_call x4, Pallas kernels, attend_chunk(): pl.pallas_call(functools.partial(attend_kernel, start=chunk * rows, rows=...  61.3 us
    unnamed x53, local copies, waits for them, and re-layouts  58.5 us
  transfers between devices with their start and end apart: 36, of which 11 were waited for; matrix products, arithmetic and copies ran while one was open for 26% of the time, Pallas kernels for 43%

profile of v1, /device:TPU:104, one launch (start us, length us, event | category | flops | bytes accessed | tf_op | source)
XLA Modules:
  0.0 917.0 jit_solution(18336707511377272140)
XLA Ops:
  11.1 31.1 %copy.29 = bf16[1,4096,2,6,128]{1,4,3,2,0:T(8,128)(2,1)} copy(bf16[1,4096,2,6,128]{4,2,3,1,0:T(2,128)(2,1)} %param.23) | data formatting | bytes 25165824 | tf_op args[8]
  55.3 34.7 %fusion.10.refs_0_.refs_1_.refs_2_.refs_3_.q_ref.v_ref = bf16[2048,1536]{1,0:T(8,128)(2,1)} fusion(bf16[4096,1536]{0,1:T(8,128)(2,1)} %bitcast.198, bf16[1,2048,4096]{2,1,0:T(8,128)(2,1)} %param.15, f32[4096]{0:T(1024)S(1)} %bitcast.216, f32[2048]{0:T(1024)S(1)} %add_rsqrt_fusion), kind=kOutput, calls=%fused_computation.16 | convolution fusion | flops 25806503936 | bytes 35676160 | tf_op jit(solution)/shard_map/dot_general | solution.py:42
  95.1 13.2 %attend.5 = bf16[512,1024]{1,0:T(8,128)(2,1)} custom-call(s32[1]{0:T(128)S(6)} %copy.70.slen_ref, bf16[2048,1536]{1,0:T(8,128)(2,1)} %fusion.10.refs_0_.refs_1_.refs_2_.refs_3_.q_ref.v_ref, f32[2048,128]{1,0:T(8,128)} %get-tuple-element.79.refs_4_.cos_ref, f32[2048,128]{1,0:T(8,128)} %get-tuple-element.80.refs_5_.sin_ref, ...), custom_call_target="tpu_custom_call" | custom-call | flops 6442450944 | bytes 2097152 | tf_op jit(solution)/shard_map/attend/pallas_call | solution.py:120
  108.7 17.1 %attend.6 = bf16[512,1024]{1,0:T(8,128)(2,1)} custom-call(s32[1]{0:T(128)S(6)} %copy.70.slen_ref, bf16[2048,1536]{1,0:T(8,128)(2,1)} %fusion.10.refs_0_.refs_1_.refs_2_.refs_3_.q_ref.v_ref, f32[2048,128]{1,0:T(8,128)} %get-tuple-element.79.refs_4_.cos_ref, f32[2048,128]{1,0:T(8,128)} %get-tuple-element.80.refs_5_.sin_ref, ...), custom_call_target="tpu_custom_call" | custom-call | flops 9663676416 | bytes 2097152 | tf_op jit(solution)/shard_map/attend/pallas_call | solution.py:120
  126.0 10.6 %attend.4.refs_0_ = bf16[512,1024]{1,0:T(8,128)(2,1)} custom-call(s32[1]{0:T(128)S(6)} %copy.70.slen_ref, bf16[2048,1536]{1,0:T(8,128)(2,1)} %fusion.10.refs_0_.refs_1_.refs_2_.refs_3_.q_ref.v_ref, f32[2048,128]{1,0:T(8,128)} %get-tuple-element.79.refs_4_.cos_ref, f32[2048,128]{1,0:T(8,128)} %get-tuple-element.80.refs_5_.sin_ref, ...), custom_call_target="tpu_custom_call" | custom-call | flops 3221225472 | bytes 2097152 | tf_op jit(solution)/shard_map/attend/pallas_call | solution.py:120
  139.4 45.9 %collective-permute-done.1.refs_4_ = bf16[512,1024]{1,0:T(8,128)(2,1)S(1)} collective-permute-done((bf16[512,1024]{1,0:T(8,128)(2,1)}, bf16[512,1024]{1,0:T(8,128)(2,1)S(1)}, u32[]{:S(2)}, u32[]{:S(2)}) %collective-permute-start.1) | collective-permute-done | bytes 1048608 | tf_op jit(solution)/shard_map/ppermute | solution.py:240
  190.2 20.4 %attend.7 = bf16[512,1024]{1,0:T(8,128)(2,1)} custom-call(s32[1]{0:T(128)S(6)} %copy.70.slen_ref, bf16[2048,1536]{1,0:T(8,128)(2,1)} %fusion.10.refs_0_.refs_1_.refs_2_.refs_3_.q_ref.v_ref, f32[2048,128]{1,0:T(8,128)} %get-tuple-element.79.refs_4_.cos_ref, f32[2048,128]{1,0:T(8,128)} %get-tuple-element.80.refs_5_.sin_ref, ...), custom_call_target="tpu_custom_call" | custom-call | flops 12884901888 | bytes 2097152 | tf_op jit(solution)/shard_map/attend/pallas_call | solution.py:120
  210.8 22.1 %project.4.h_ref = bf16[512,4096]{1,0:T(8,128)(2,1)S(1)} custom-call(s32[1]{0:T(128)} %bitcast.place_ref, bf16[512,1024]{1,0:T(8,128)(2,1)S(1)} %copy-done, bf16[512,1024]{1,0:T(8,128)(2,1)S(1)} %collective-permute-done.refs_1_, bf16[256,1024]{1,0:T(8,128)(2,1)} %collective-permute-done.2.refs_2_, bf16[256,1024]{1,0:T(8,128)(2,1)} %collective-permute-done.3.refs_3_, ...), custom_call_target="tpu_custom_call" | custom-call | flops 17179869184 | bytes 33554432 | tf_op jit(solution)/shard_map/project/pallas_call | solution.py:167
  235.0 61.0 %mlp.4 = f32[512,4096]{1,0:T(8,128)} custom-call(bf16[512,4096]{1,0:T(8,128)(2,1)} %copy-done.2, bf16[1,4096]{1,0:T(2,128)(2,1)} %gain_ref.7, bf16[4096,3584]{1,0:T(8,128)(2,1)} %bitcast.190, bf16[4096,3584]{1,0:T(8,128)(2,1)} %bitcast.182, bf16[3584,4096]{1,0:T(8,128)(2,1)} %bitcast.186), custom_call_target="tpu_custom_call" | custom-call | flops 45097156608 | bytes 88080384 | tf_op jit(solution)/shard_map/mlp/pallas_call | solution.py:214
  302.3 21.7 %project.5.h_ref = bf16[512,4096]{1,0:T(8,128)(2,1)S(1)} custom-call(s32[1]{0:T(128)} %bitcast.place_ref, bf16[4,512,1024]{2,1,0:T(8,128)(2,1)S(1)} %bitcast.181, bf16[4096,4096]{1,0:T(8,128)(2,1)} %all-gather.12.cloned.1.call-done.refs_5_.refs_1_, bf16[2048,4096]{1,0:T(8,128)(2,1)} %bitcast.195), custom_call_target="tpu_custom_call" | custom-call | flops 17179869184 | bytes 33554432 | tf_op jit(solution)/shard_map/project/pallas_call | solution.py:167
  330.8 61.3 %mlp.5 = f32[512,4096]{1,0:T(8,128)} custom-call(bf16[512,4096]{1,0:T(8,128)(2,1)} %copy-done.1, bf16[1,4096]{1,0:T(2,128)(2,1)} %gain_ref.7, bf16[4096,3584]{1,0:T(8,128)(2,1)} %bitcast.191, bf16[4096,3584]{1,0:T(8,128)(2,1)} %bitcast.183, bf16[3584,4096]{1,0:T(8,128)(2,1)} %bitcast.187), custom_call_target="tpu_custom_call" | custom-call | flops 45097156608 | bytes 88080384 | tf_op jit(solution)/shard_map/mlp/pallas_call | solution.py:214
  408.4 36.1 %collective-permute-done.10 = f32[64,4096]{1,0:T(8,128)} collective-permute-done((f32[64,4096]{1,0:T(8,128)}, f32[64,4096]{1,0:T(8,128)}, u32[]{:S(2)}, u32[]{:S(2)}) %collective-permute-start.10) | collective-permute-done | bytes 1048608 | tf_op jit(solution)/shard_map/ppermute | solution.py:240
  451.7 39.3 %collective-permute-done.5 = f32[128,4096]{1,0:T(8,128)} collective-permute-done((f32[128,4096]{1,0:T(8,128)}, f32[128,4096]{1,0:T(8,128)}, u32[]{:S(2)}, u32[]{:S(2)}) %collective-permute-start.5) | collective-permute-done | bytes 2097184 | tf_op jit(solution)/shard_map/ppermute | solution.py:240
  501.4 21.9 %project.6.h_ref = bf16[512,4096]{1,0:T(8,128)(2,1)S(1)} custom-call(s32[1]{0:T(128)} %bitcast.place_ref, bf16[4,512,1024]{2,1,0:T(8,128)(2,1)S(1)} %bitcast.180, bf16[4096,4096]{1,0:T(8,128)(2,1)} %all-gather.12.cloned.1.call-done.refs_5_.refs_1_, bf16[2048,4096]{1,0:T(8,128)(2,1)} %bitcast.196), custom_call_target="tpu_custom_call" | custom-call | flops 17179869184 | bytes 33554432 | tf_op jit(solution)/shard_map/project/pallas_call | solution.py:167
  525.4 61.1 %mlp.6 = f32[512,4096]{1,0:T(8,128)} custom-call(bf16[512,4096]{1,0:T(8,128)(2,1)} %copy-done.4, bf16[1,4096]{1,0:T(2,128)(2,1)} %gain_ref.7, bf16[4096,3584]{1,0:T(8,128)(2,1)} %bitcast.192, bf16[4096,3584]{1,0:T(8,128)(2,1)} %bitcast.184, bf16[3584,4096]{1,0:T(8,128)(2,1)} %bitcast.188), custom_call_target="tpu_custom_call" | custom-call | flops 45097156608 | bytes 88080384 | tf_op jit(solution)/shard_map/mlp/pallas_call | solution.py:214
  599.9 9.5 %collective-permute-done.14 = f32[64,4096]{1,0:T(8,128)} collective-permute-done((f32[64,4096]{1,0:T(8,128)}, f32[64,4096]{1,0:T(8,128)}, u32[]{:S(2)}, u32[]{:S(2)}) %collective-permute-start.14) | collective-permute-done | bytes 1048608 | tf_op jit(solution)/shard_map/ppermute | solution.py:240
  617.7 21.7 %project.7.h_ref = bf16[512,4096]{1,0:T(8,128)(2,1)S(1)} custom-call(s32[1]{0:T(128)} %bitcast.place_ref, bf16[4,512,1024]{2,1,0:T(8,128)(2,1)S(1)} %bitcast.179, bf16[4096,4096]{1,0:T(8,128)(2,1)} %all-gather.12.cloned.1.call-done.refs_5_.refs_1_, bf16[2048,4096]{1,0:T(8,128)(2,1)} %bitcast.197), custom_call_target="tpu_custom_call" | custom-call | flops 17179869184 | bytes 33554432 | tf_op jit(solution)/shard_map/project/pallas_call | solution.py:167
  641.4 61.3 %mlp.7 = f32[512,4096]{1,0:T(8,128)} custom-call(bf16[512,4096]{1,0:T(8,128)(2,1)} %copy-done.3, bf16[1,4096]{1,0:T(2,128)(2,1)} %gain_ref.7, bf16[4096,3584]{1,0:T(8,128)(2,1)} %bitcast.193, bf16[4096,3584]{1,0:T(8,128)(2,1)} %bitcast.185, bf16[3584,4096]{1,0:T(8,128)(2,1)} %bitcast.189), custom_call_target="tpu_custom_call" | custom-call | flops 45097156608 | bytes 88080384 | tf_op jit(solution)/shard_map/mlp/pallas_call | solution.py:214
  715.7 12.7 %broadcast_select_fusion.3 = (bf16[16,512,2,128]{3,2,1,0:T(2,128)(2,1)}, bf16[16,512,2,128]{3,2,1,0:T(2,128)(2,1)}) fusion(pred[16,512]{1,0:T(8,128)(4,1)S(1)} %copy-done.15, bf16[1,1,16,512,2,128]{5,4,3,2,1,0:T(2,128)(2,1)S(1)} %copy-done.8, bf16[16,2,128]{2,1,0:T(2,128)(2,1)S(1)} %copy.31, bf16[1,1,16,512,2,128]{5,4,3,2,1,0:T(2,128)(2,1)S(1)} %copy-done.9, ...), kind=kLoop, calls=%fused_computation.15 | loop fusion | flops 4194304 | bytes 16801792 | tf_op jit(solution)/shard_map/jit(_where)/select_n | solution.py:308
  772.2 54.4 %collective-permute-done.22 = f32[1,16,4096]{2,1,0:T(8,128)S(1)} collective-permute-done((f32[1,16,4096]{2,1,0:T(8,128)S(1)}, f32[1,16,4096]{2,1,0:T(8,128)S(1)}, u32[]{:S(2)}, u32[]{:S(2)}) %collective-permute-start.22) | collective-permute-done | bytes 262176 | tf_op jit(solution)/shard_map/ppermute | solution.py:240
  835.4 11.4 %fusion.19 = f32[16,3584]{1,0:T(8,128)S(1)} fusion(bf16[1,16,4096]{2,1,0:T(8,128)(2,1)S(1)} %fusion.54, f32[4096]{0:T(1024)S(1)} %bitcast.213, f32[16]{0:T(128)S(1)} %add_rsqrt_fusion.1, bf16[1,4096,3584]{2,1,0:T(8,128)(2,1)} %param.27), kind=kOutput, calls=%fused_computation.24 | convolution fusion | flops 470138880 | bytes 29737024 | tf_op jit(solution)/shard_map/dot_general | solution.py:42
  846.8 22.7 %convolution_bitcast_fusion = f32[1,16,4096]{2,1,0:T(8,128)S(1)} fusion(f32[16,3584]{1,0:T(8,128)S(1)} %fusion.19, bf16[1,16,4096]{2,1,0:T(8,128)(2,1)S(1)} %fusion.54, f32[4096]{0:T(1024)S(1)} %bitcast.214, f32[16]{0:T(128)S(1)} %add_rsqrt_fusion.1, bf16[1,3584,4096]{2,1,0:T(8,128)(2,1)} %param.29, bf16[1,4096,3584]{2,1,0:T(8,128)(2,1)} %param.28), kind=kOutput, calls=%fused_computation.18 | convolution fusion | flops 940244992 | bytes 59359296 | tf_op jit(solution)/shard_map/dot_general | solution.py:42
  875.5 14.0 %broadcast_select_fusion = (bf16[1,1,16,512,2,128]{5,4,3,2,1,0:T(2,128)(2,1)}, bf16[1,1,16,512,2,128]{5,4,3,2,1,0:T(2,128)(2,1)}) fusion(bf16[1,1,16,512,2,128]{5,4,3,2,1,0:T(2,128)(2,1)} %param.20, pred[16,512]{1,0:T(8,128)(4,1)S(1)} %copy-done.15, bf16[16,2,128]{2,1,0:T(2,128)(2,1)S(1)} %copy.34, bf16[1,1,16,512,2,128]{5,4,3,2,1,0:T(2,128)(2,1)} %param.19, ...), kind=kLoop, calls=%fused_computation.12 | loop fusion | flops 4194304 | bytes 16801792 | tf_op jit(solution)/shard_map/jit(_where)/select_n | solution.py:309
  896.1 13.6 %maximum_bitcast_fusion = bf16[1,2048,4096]{2,1,0:T(8,128)(2,1)} fusion(bf16[512,4096]{1,0:T(8,128)(2,1)} %all-gather.20.cloned.1.call-done, bf16[512,4096]{1,0:T(8,128)(2,1)} %all-gather.18.cloned.1.call-done, bf16[512,4096]{1,0:T(8,128)(2,1)} %all-gather.16.cloned.1.call-done, bf16[512,4096]{1,0:T(8,128)(2,1)} %all-gather.14.cloned.1.call-done), kind=kLoop, calls=%fused_computation.5 | loop fusion | flops 67108864 | bytes 33554432 | tf_op jit(solution)/shard_map/broadcast_in_dim | solution.py:417
  (184 shorter events, 182.3 us)
Async XLA Ops:
  7.2 203.6 %all-gather.12.cloned.1.call-start = ((), (), s32[]{:S(2)}) async-start(), calls=%async_computation | async-start | bytes 34603008 | tf_op jit(solution)/shard_map/all_gather | solution.py:370
  9.6 286.4 %all-gather.22.cloned.1.call-start = ((), (), s32[]{:S(2)}) async-start(), calls=%async_computation.5 | async-start | bytes 5242880 | tf_op jit(solution)/shard_map/all_gather | solution.py:384
  108.3 390.9 %all-gather.24.cloned.1.call-start = ((), (), s32[]{:S(2)}) async-start(), calls=%async_computation.6 | async-start | bytes 5242880 | tf_op jit(solution)/shard_map/all_gather | solution.py:384
  125.9 473.9 %all-gather.26.cloned.1.call-start = ((), (), s32[]{:S(2)}) async-start(), calls=%async_computation.7 | async-start | bytes 5242880 | tf_op jit(solution)/shard_map/all_gather | solution.py:384
  136.6 48.7 %collective-permute-start.1 = (bf16[512,1024]{1,0:T(8,128)(2,1)}, bf16[512,1024]{1,0:T(8,128)(2,1)S(1)}, u32[]{:S(2)}, u32[]{:S(2)}) collective-permute-start(bf16[512,1024]{1,0:T(8,128)(2,1)} %attend.4.refs_0_), channel_id=1, source_target_pairs={{0,8},{8,16},{16,24},{24,0},{1,9},{9,17},{17,25},{25,1},{2,10},{10... | collective-permute-start | bytes 3145736 | tf_op jit(solution)/shard_map/ppermute | solution.py:240
  139.4 49.1 %collective-permute-start = (bf16[512,1024]{1,0:T(8,128)(2,1)}, bf16[512,1024]{1,0:T(8,128)(2,1)S(1)}, u32[]{:S(2)}, u32[]{:S(2)}) collective-permute-start(bf16[512,1024]{1,0:T(8,128)(2,1)} %attend.4.refs_0_), channel_id=1, source_target_pairs={{8,0},{16,8},{24,16},{0,24},{9,1},{17,9},{25,17},{1,25},{10,2},{18... | collective-permute-start | bytes 3145736 | tf_op jit(solution)/shard_map/ppermute | solution.py:240
  210.7 683.1 %all-gather.14.cloned.1.call-start = ((), (), s32[]{:S(2)}) async-start(), calls=%async_computation.1 | async-start | bytes 5242880 | tf_op jit(solution)/shard_map/all_gather | solution.py:413
  395.6 48.9 %collective-permute-start.10 = (f32[64,4096]{1,0:T(8,128)}, f32[64,4096]{1,0:T(8,128)}, u32[]{:S(2)}, u32[]{:S(2)}) collective-permute-start(f32[64,4096]{1,0:T(8,128)} %get-tuple-element.45), channel_id=1, source_target_pairs={{8,0},{16,8},{24,16},{0,24},{9,1},{17,9},{25,17},{1,25},{10,2},{18... | collective-permute-start | bytes 3145736 | tf_op jit(solution)/shard_map/ppermute | solution.py:240
  400.8 189.6 %collective-permute-start.26 = (bf16[2,2048,128]{2,1,0:T(8,128)(2,1)}, bf16[2,2048,128]{2,1,0:T(8,128)(2,1)}, u32[]{:S(2)}, u32[]{:S(2)}) collective-permute-start(bf16[2,2048,128]{2,1,0:T(8,128)(2,1)} %get-tuple-element.58), channel_id=1, source_target_pairs={{0,4},{8,20},{16,12},{24,28},{1,5},{9,21},{17,13},{25,29},{2,6},{1... | collective-permute-start | bytes 3145736 | tf_op jit(solution)/shard_map/ppermute | solution.py:300
  405.0 86.0 %collective-permute-start.5 = (f32[128,4096]{1,0:T(8,128)}, f32[128,4096]{1,0:T(8,128)}, u32[]{:S(2)}, u32[]{:S(2)}) collective-permute-start(f32[128,4096]{1,0:T(8,128)} %pad_maximum_fusion), channel_id=1, source_target_pairs={{0,8},{8,16},{16,24},{24,0},{1,9},{9,17},{17,25},{25,1},{2,10},{10... | collective-permute-start | bytes 6291464 | tf_op jit(solution)/shard_map/ppermute | solution.py:240
  406.6 87.4 %collective-permute-start.7 = (f32[128,4096]{1,0:T(8,128)}, f32[128,4096]{1,0:T(8,128)}, u32[]{:S(2)}, u32[]{:S(2)}) collective-permute-start(f32[128,4096]{1,0:T(8,128)} %pad_maximum_fusion.1), channel_id=1, source_target_pairs={{8,0},{16,8},{24,16},{0,24},{9,1},{17,9},{25,17},{1,25},{10,2},{18... | collective-permute-start | bytes 6291464 | tf_op jit(solution)/shard_map/ppermute | solution.py:240
  444.5 147.9 %collective-permute-start.27 = (bf16[2,2048,128]{2,1,0:T(8,128)(2,1)}, bf16[2,2048,128]{2,1,0:T(8,128)(2,1)}, u32[]{:S(2)}, u32[]{:S(2)}) collective-permute-start(bf16[2,2048,128]{2,1,0:T(8,128)(2,1)} %get-tuple-element.59), channel_id=1, source_target_pairs={{0,12},{8,28},{16,4},{24,20},{1,13},{9,29},{17,5},{25,21},{2,14},{... | collective-permute-start | bytes 3145736 | tf_op jit(solution)/shard_map/ppermute | solution.py:300
  448.4 146.6 %collective-permute-start.9 = (f32[128,4096]{1,0:T(8,128)}, f32[128,4096]{1,0:T(8,128)}, u32[]{:S(2)}, u32[]{:S(2)}) collective-permute-start(f32[128,4096]{1,0:T(8,128)} %pad_maximum_fusion.2), channel_id=1, source_target_pairs={{0,8},{8,16},{16,24},{24,0},{1,9},{9,17},{17,25},{25,1},{2,10},{10... | collective-permute-start | bytes 6291464 | tf_op jit(solution)/shard_map/ppermute | solution.py:240
  491.0 104.0 %collective-permute-start.11 = (f32[128,4096]{1,0:T(8,128)}, f32[128,4096]{1,0:T(8,128)}, u32[]{:S(2)}, u32[]{:S(2)}) collective-permute-start(f32[128,4096]{1,0:T(8,128)} %pad_maximum_fusion.3), channel_id=1, source_target_pairs={{8,0},{16,8},{24,16},{0,24},{9,1},{17,9},{25,17},{1,25},{10,2},{18... | collective-permute-start | bytes 6291464 | tf_op jit(solution)/shard_map/ppermute | solution.py:240
  498.7 395.0 %all-gather.16.cloned.1.call-start = ((), (), s32[]{:S(2)}) async-start(), calls=%async_computation.2 | async-start | bytes 5242880 | tf_op jit(solution)/shard_map/all_gather | solution.py:413
  599.8 294.0 %all-gather.18.cloned.1.call-start = ((), (), s32[]{:S(2)}) async-start(), calls=%async_computation.3 | async-start | bytes 5242880 | tf_op jit(solution)/shard_map/all_gather | solution.py:413
  613.7 114.6 %collective-permute-start.13 = (f32[128,4096]{1,0:T(8,128)}, f32[128,4096]{1,0:T(8,128)}, u32[]{:S(2)}, u32[]{:S(2)}) collective-permute-start(f32[128,4096]{1,0:T(8,128)} %pad_maximum_fusion.4), channel_id=1, source_target_pairs={{0,8},{8,16},{16,24},{24,0},{1,9},{9,17},{17,25},{25,1},{2,10},{10... | collective-permute-start | bytes 6291464 | tf_op jit(solution)/shard_map/ppermute | solution.py:240
  617.5 110.8 %collective-permute-start.15 = (f32[128,4096]{1,0:T(8,128)}, f32[128,4096]{1,0:T(8,128)}, u32[]{:S(2)}, u32[]{:S(2)}) collective-permute-start(f32[128,4096]{1,0:T(8,128)} %pad_maximum_fusion.5), channel_id=1, source_target_pairs={{8,0},{16,8},{24,16},{0,24},{9,1},{17,9},{25,17},{1,25},{10,2},{18... | collective-permute-start | bytes 6291464 | tf_op jit(solution)/shard_map/ppermute | solution.py:240
  733.1 163.1 %all-gather.20.cloned.1.call-start = ((), (), s32[]{:S(2)}) async-start(), calls=%async_computation.4 | async-start | bytes 5242880 | tf_op jit(solution)/shard_map/all_gather | solution.py:413
  743.4 88.4 %collective-permute-start.17 = (f32[128,4096]{1,0:T(8,128)S(1)}, f32[128,4096]{1,0:T(8,128)S(1)}, u32[]{:S(2)}, u32[]{:S(2)}) collective-permute-start(f32[128,4096]{1,0:T(8,128)S(1)} %pad_maximum_fusion.6), channel_id=1, source_target_pairs={{0,8},{8,16},{16,24},{24,0},{1,9},{9,17},{17,25},{25,1},{2,10},{10... | collective-permute-start | bytes 6291464 | tf_op jit(solution)/shard_map/ppermute | solution.py:240
  745.6 86.2 %collective-permute-start.19 = (f32[128,4096]{1,0:T(8,128)S(1)}, f32[128,4096]{1,0:T(8,128)S(1)}, u32[]{:S(2)}, u32[]{:S(2)}) collective-permute-start(f32[128,4096]{1,0:T(8,128)S(1)} %pad_maximum_fusion.7), channel_id=1, source_target_pairs={{8,0},{16,8},{24,16},{0,24},{9,1},{17,9},{25,17},{1,25},{10,2},{18... | collective-permute-start | bytes 6291464 | tf_op jit(solution)/shard_map/ppermute | solution.py:240
  747.6 79.1 %collective-permute-start.22 = (f32[1,16,4096]{2,1,0:T(8,128)S(1)}, f32[1,16,4096]{2,1,0:T(8,128)S(1)}, u32[]{:S(2)}, u32[]{:S(2)}) collective-permute-start(f32[1,16,4096]{2,1,0:T(8,128)S(1)} %fusion.13), channel_id=1, source_target_pairs={{8,0},{16,8},{24,16},{0,24},{9,1},{17,9},{25,17},{1,25},{10,2},{18... | collective-permute-start | bytes 786440 | tf_op jit(solution)/shard_map/ppermute | solution.py:240
  750.8 76.0 %collective-permute-start.21 = (f32[1,16,4096]{2,1,0:T(8,128)S(1)}, f32[1,16,4096]{2,1,0:T(8,128)S(1)}, u32[]{:S(2)}, u32[]{:S(2)}) collective-permute-start(f32[1,16,4096]{2,1,0:T(8,128)S(1)} %fusion.13), channel_id=1, source_target_pairs={{0,8},{8,16},{16,24},{24,0},{1,9},{9,17},{17,25},{25,1},{2,10},{10... | collective-permute-start | bytes 786440 | tf_op jit(solution)/shard_map/ppermute | solution.py:240
  751.0 80.6 %collective-permute-start.20 = (f32[1,16,4096]{2,1,0:T(8,128)S(1)}, f32[1,16,4096]{2,1,0:T(8,128)S(1)}, u32[]{:S(2)}, u32[]{:S(2)}) collective-permute-start(f32[1,16,4096]{2,1,0:T(8,128)S(1)} %fusion.13), channel_id=1, source_target_pairs={{0,16},{8,24},{16,0},{24,8},{1,17},{9,25},{17,1},{25,9},{2,18},{10... | collective-permute-start | bytes 786440 | tf_op jit(solution)/shard_map/ppermute | solution.py:283
  (37 other events, 605.8 us)
Sparse Core Ops, SparseCore 0:
  10.7 110.2 all-gather.11
  123.1 67.6 all-gather.21
  192.3 45.9 all-gather.23
  239.8 47.3 all-gather.25
  498.8 68.0 all-gather.13
  599.9 75.9 all-gather.15
  733.2 82.9 all-gather.17
  835.5 60.6 all-gather.19

commit v2 on v1

--- a/solution.py
+++ b/solution.py
@@ -9,9 +9,14 @@
 
 NORM_EPS = 1e-5
 ROPE_BASE = 10000.0
-CHUNKS = 4
+EDGE_ROWS = 256
+MID_ROWS = 512
 F32 = jnp.float32
 BF16 = jnp.bfloat16
+
+
+def chunk_edges(seq_len):
+    return [0] + list(range(EDGE_ROWS, seq_len, MID_ROWS)) + [seq_len]
 
 
 def rope_tables(positions, head_dim):
@@ -77,14 +82,15 @@
     )(s_len, *([qkv] * (2 * kv_local)), cos_full, sin_full)
 
 
-def attend_kernel(slen_ref, q_ref, cos_ref, sin_ref, k_ref, v_ref, out_ref, *, start, rows, sub):
-    head_dim = q_ref.shape[1]
+def attend_kernel(slen_ref, *refs, start, sub, n_q):
+    q_refs, cos_refs, sin_refs = refs[:n_q], refs[n_q:2 * n_q], refs[2 * n_q:3 * n_q]
+    k_ref, v_ref, out_ref = refs[3 * n_q:]
+    head_dim = k_ref.shape[1]
     scale = (head_dim ** -0.5) * math.log2(math.e)
-    q32 = q_ref[...].astype(F32)
-    q_rot = (q32 * cos_ref[...] + pltpu.roll(q32, head_dim // 2, 1) * sin_ref[...]).astype(BF16)
     dims = (((1,), (1,)), ((), ()))
-    for part in range(rows // sub):
-        q_part = q_rot[part * sub:(part + 1) * sub]
+    for part in range(n_q):
+        q32 = q_refs[part][...].astype(F32)
+        q_part = (q32 * cos_refs[part][...] + pltpu.roll(q32, head_dim // 2, 1) * sin_refs[part][...]).astype(BF16)
         base = start + part * sub
         width = base + sub
         tail = lax.dot_general(q_part, k_ref[base:width], dims, preferred_element_type=F32)
@@ -112,19 +118,19 @@
         out_ref[part * sub:(part + 1) * sub, :] = acc.astype(BF16)
 
 
-def attend_chunk(qkv, k_rot, cos_full, sin_full, s_len, chunk, rows, kv_local, group_size, head_dim):
+def attend_chunk(qkv, k_rot, cos_full, sin_full, s_len, start, rows, kv_local, group_size, head_dim, sub=256):
     heads = kv_local * group_size
     per_kv = group_size + 2
-    width = (chunk + 1) * rows
-    tab = pl.BlockSpec((rows, head_dim), lambda h: (chunk, 0))
+    width = start + rows
+    n_q = rows // sub
+    first = start // sub
+    tabs = [pl.BlockSpec((sub, head_dim), lambda h, r=r: (first + r, 0)) for r in range(n_q)]
     return pl.pallas_call(
-        functools.partial(attend_kernel, start=chunk * rows, rows=rows, sub=256),
+        functools.partial(attend_kernel, start=start, sub=sub, n_q=n_q),
         grid=(heads,),
-        in_specs=[
-            pl.BlockSpec(memory_space=pltpu.SMEM),
-            pl.BlockSpec((rows, head_dim), lambda h: (chunk, (h // group_size) * per_kv + h % group_size)),
-            tab,
-            tab,
+        in_specs=[pl.BlockSpec(memory_space=pltpu.SMEM)]
+        + [pl.BlockSpec((sub, head_dim), lambda h, r=r: (first + r, (h // group_size) * per_kv + h % group_size)) for r in range(n_q)]
+        + tabs + tabs + [
             pl.BlockSpec((width, head_dim), lambda h: (0, h // group_size)),
             pl.BlockSpec((width, head_dim), lambda h: (0, (h // group_size) * per_kv + group_size + 1)),
         ],
@@ -132,12 +138,14 @@
         out_shape=jax.ShapeDtypeStruct((rows, heads * head_dim), BF16),
         cost_estimate=pl.CostEstimate(flops=4 * rows * width * heads * head_dim * 3, bytes_accessed=4 * rows * heads * head_dim, transcendentals=rows * width * heads),
         name="attend",
-    )(s_len, qkv, cos_full, sin_full, k_rot, qkv)
-
-
-def project_kernel(place_ref, *refs, tp_count, n_in):
+    )(s_len, *([qkv] * n_q), *([cos_full] * n_q), *([sin_full] * n_q), k_rot, qkv)
+
+
+def project_kernel(place_ref, *refs, tp_count, n_in, n_x):
     ctx_refs = refs[:n_in]
-    w_ref, x_ref, h_ref, ctx_all = refs[n_in:]
+    w_ref = refs[n_in]
+    x_refs = refs[n_in + 1:n_in + 1 + n_x]
+    h_ref, ctx_all = refs[n_in + 1 + n_x:]
 
     @pl.when(pl.program_id(0) == 0)
     def _():
@@ -157,42 +165,56 @@
     acc = dot32(ctx_all[0], w_ref[:depth])
     for block in range(1, tp_count):
         acc += dot32(ctx_all[block], w_ref[block * depth:(block + 1) * depth])
-    h_ref[...] = (x_ref[...].astype(F32) + acc.astype(BF16).astype(F32)).astype(BF16)
-
-
-def project_chunk(ctx_parts, out_full, x, row_block, rows, place, tp_count, tile=512):
+    sub = x_refs[0].shape[0]
+    for part in range(n_x):
+        at = slice(part * sub, (part + 1) * sub)
+        h_ref[at] = (x_refs[part][...].astype(F32) + acc[at].astype(BF16).astype(F32)).astype(BF16)
+
+
+def project_chunk(ctx_parts, out_full, x, start, rows, place, tp_count, tile=512, sub=256):
     full_depth, width = out_full.shape
     depth = full_depth // tp_count
+    n_x = rows // sub
+    first = start // sub
     whole = lambda part: pl.BlockSpec(part.shape, lambda j: (0,) * part.ndim, pipeline_mode=pl.Buffered(1))
     return pl.pallas_call(
-        functools.partial(project_kernel, tp_count=tp_count, n_in=len(ctx_parts)),
+        functools.partial(project_kernel, tp_count=tp_count, n_in=len(ctx_parts), n_x=n_x),
         grid=(width // tile,),
         in_specs=[pl.BlockSpec(memory_space=pltpu.SMEM)] + [whole(p) for p in ctx_parts] + [
             pl.BlockSpec((full_depth, tile), lambda j: (0, j)),
-            pl.BlockSpec((rows, tile), lambda j: (row_block, j)),
-        ],
+        ] + [pl.BlockSpec((sub, tile), lambda j, r=r: (first + r, j)) for r in range(n_x)],
         out_specs=pl.BlockSpec((rows, tile), lambda j: (0, j)),
         out_shape=jax.ShapeDtypeStruct((rows, width), BF16),
         scratch_shapes=[pltpu.VMEM((tp_count, rows, depth), BF16)],
         compiler_params=pltpu.CompilerParams(vmem_limit_bytes=40 * 1024 * 1024),
         cost_estimate=pl.CostEstimate(flops=2 * rows * full_depth * width, bytes_accessed=2 * full_depth * width, transcendentals=0),
         name="project",
-    )(place, *ctx_parts, out_full, x)
-
-
-def mlp_kernel(h_ref, gain_ref, wg_ref, wu_ref, wd_ref, out_ref, m_ref):
+    )(place, *ctx_parts, out_full, *([x] * n_x))
+
+
+def mlp_kernel(place_ref, h_ref, gain_ref, wg_ref, wu_ref, wd_ref, *refs, tp_count, extra):
+    refs = list(refs)
+    extra_ref = refs.pop(0) if extra else None
+    m_ref = refs.pop()
     step = pl.program_id(0)
     rows, _ = h_ref.shape
-    sub = min(rows, 128)
+    block = rows // tp_count
+    me = place_ref[0]
+
+    def norm(h):
+        h32 = h.astype(F32)
+        inv_rms = lax.rsqrt(jnp.mean(h32 * h32, axis=-1, keepdims=True) + NORM_EPS)
+        return (h32 * inv_rms * gain_ref[...].astype(F32)).astype(BF16)
 
     @pl.when(step == 0)
     def _():
-        @pl.loop(0, rows // sub)
-        def _(part):
-            at = pl.ds(pl.multiple_of(part * sub, sub), sub)
-            h32 = h_ref[at, :].astype(F32)
-            inv_rms = lax.rsqrt(jnp.mean(h32 * h32, axis=-1, keepdims=True) + NORM_EPS)
-            m_ref[at, :] = (h32 * inv_rms * gain_ref[...].astype(F32)).astype(BF16)
+        @pl.loop(0, tp_count)
+        def _(dist):
+            source = lax.rem(me + dist, tp_count) * block
+            m_ref[pl.ds(pl.multiple_of(dist * block, block), block), :] = norm(h_ref[pl.ds(pl.multiple_of(source, block), block), :])
+
+        if extra:
+            m_ref[rows:, :] = norm(extra_ref[...])
 
     gate_act = dot32(m_ref[...], wg_ref[...]).astype(BF16).astype(F32)
     up_proj = dot32(m_ref[...], wu_ref[...]).astype(BF16).astype(F32)
@@ -200,34 +222,53 @@
 
     @pl.when(step == 0)
     def _():
-        out_ref[...] = dot32(swi_act, wd_ref[...])
+        part = dot32(swi_act, wd_ref[...])
+        at = 0
+        for ref in refs:
+            ref[...] = part[at:at + ref.shape[0]]
+            at += ref.shape[0]
 
     @pl.when(step > 0)
     def _():
-        out_ref[...] += dot32(swi_act, wd_ref[...])
-
-
-def mlp_chunk(hidden, gain, gate_mat, up_mat, down_mat, tile=512):
+        part = dot32(swi_act, wd_ref[...])
+        at = 0
+        for ref in refs:
+            ref[...] += part[at:at + ref.shape[0]]
+            at += ref.shape[0]
+
+
+def mlp_chunk(hidden, gain, gate_mat, up_mat, down_mat, place, tp_count, extra=None, tile=512):
     rows, width = hidden.shape
     ff = gate_mat.shape[1]
+    block = rows // tp_count
+    sizes = [block, block, block // 2, block // 2, block]
+    total = rows
+    operands = [place, hidden, gain, gate_mat, up_mat, down_mat]
     once = lambda shape: pl.BlockSpec(shape, lambda f: (0, 0), pipeline_mode=pl.Buffered(1))
+    in_specs = [
+        pl.BlockSpec(memory_space=pltpu.SMEM),
+        once((rows, width)),
+        once((1, width)),
+        pl.BlockSpec((width, tile), lambda f: (0, f)),
+        pl.BlockSpec((width, tile), lambda f: (0, f)),
+        pl.BlockSpec((tile, width), lambda f: (f, 0)),
+    ]
+    if extra is not None:
+        sizes.append(extra.shape[0])
+        total += extra.shape[0]
+        operands.append(extra)
+        in_specs.append(once(extra.shape))
     return pl.pallas_call(
-        mlp_kernel,
+        functools.partial(mlp_kernel, tp_count=tp_count, extra=extra is not None),
         grid=(ff // tile,),
-        in_specs=[
-            once((rows, width)),
-            once((1, width)),
-            pl.BlockSpec((width, tile), lambda f: (0, f)),
-            pl.BlockSpec((width, tile), lambda f: (0, f)),
-            pl.BlockSpec((tile, width), lambda f: (f, 0)),
-        ],
-        out_specs=pl.BlockSpec((rows, width), lambda f: (0, 0), pipeline_mode=pl.Buffered(1)),
-        out_shape=jax.ShapeDtypeStruct((rows, width), F32),
-        scratch_shapes=[pltpu.VMEM((rows, width), BF16)],
+        in_specs=in_specs,
+        out_specs=[once((size, width)) for size in sizes],
+        out_shape=[jax.ShapeDtypeStruct((size, width), F32) for size in sizes],
+        scratch_shapes=[pltpu.VMEM((total, width), BF16)],
         compiler_params=pltpu.CompilerParams(vmem_limit_bytes=60 * 1024 * 1024),
         cost_estimate=pl.CostEstimate(flops=6 * rows * width * ff, bytes_accessed=6 * width * ff, transcendentals=rows * ff),
         name="mlp",
-    )(hidden, gain, gate_mat, up_mat, down_mat)
+    )(*operands)
 
 
 def after(value, *deps):
@@ -245,34 +286,29 @@
     half = block.shape[0] // 2
     prev = send_up(block)
     succ = send_down(block)
-    return [block, succ, send_up(prev[:half]), send_down(succ[half:]), prev]
-
-
-def scatter_first(partial, tp_count, me):
+    far_a = send_up(prev[:half])
+    far_b = send_down(succ[half:])
+    return [block, succ, far_a, far_b, prev]
+
+
+def scatter_first(parts, tp_count):
     send_up, send_down = make_ring(tp_count)
-    half = partial.shape[1] // 2
-    far_at = (me + 2) % tp_count
-    width = partial.shape[2]
-    lower = lax.dynamic_slice(partial, (far_at, 0, 0), (1, half, width))[0]
-    upper = lax.dynamic_slice(partial, (far_at, half, 0), (1, half, width))[0]
-    from_prev = send_up(lower)
-    from_succ = send_down(upper)
+    from_prev = send_up(parts[2])
+    from_succ = send_down(parts[3])
     return from_prev, from_succ
 
 
-def scatter_add(partial, first, tp_count, me):
+def scatter_add(parts, first):
     from_prev, from_succ = first
-    half = partial.shape[1] // 2
-    pick = lambda dist: lax.dynamic_index_in_dim(partial, (me + dist) % tp_count, axis=0, keepdims=False)
-    succ, prev = pick(1), pick(3)
-    up_block = jnp.concatenate([succ[:half] + from_prev, succ[half:]], axis=0)
-    down_block = jnp.concatenate([prev[:half], prev[half:] + from_succ], axis=0)
+    succ, prev = parts[1], parts[4]
+    half = from_prev.shape[0]
+    up_block = lax.dynamic_update_slice(succ, succ[:half] + from_prev, (0, 0))
+    down_block = lax.dynamic_update_slice(prev, prev[half:] + from_succ, (half, 0))
     return up_block, down_block
 
 
-def scatter_last(partial, blocks, tp_count, me):
+def scatter_last(own, blocks, tp_count):
     send_up, send_down = make_ring(tp_count)
-    own = lax.dynamic_index_in_dim(partial, me, axis=0, keepdims=False)
     from_prev = send_up(blocks[0])
     from_succ = send_down(blocks[1])
     return own + (from_prev + from_succ)
@@ -281,7 +317,9 @@
 def small_sum(partial, tp_count):
     send_up, send_down = make_ring(tp_count)
     far = lax.ppermute(partial, 'tp', [(i, (i + 2) % tp_count) for i in range(tp_count)])
-    return (partial + far) + (send_up(partial) + send_down(partial))
+    prev = send_up(partial)
+    succ = send_down(partial)
+    return (partial + far) + (prev + succ)
 
 
 def hand_off(pack, tp_count, node_count, tp_index):
@@ -304,25 +342,20 @@
     return both[0][None, None], both[1][None, None]
 
 
+def write_cache(old, new, write_mask):
+    return jnp.where(write_mask[:, :, :, None, None], new[:, :, None], old)
+
+
 def decode_attention(q_rot, k_rot, v_new, k_old, v_old, write_mask, seen_mask):
-    k_upd = jnp.where(write_mask[:, :, :, None, None], k_rot[:, :, None], k_old)
-    v_upd = jnp.where(write_mask[:, :, :, None, None], v_new[:, :, None], v_old)
+    k_upd = write_cache(k_old, k_rot, write_mask)
+    v_upd = write_cache(v_old, v_new, write_mask)
     scores = jnp.einsum('nbkgd,nbtkd->nbkgt', q_rot, k_upd, preferred_element_type=F32) * (q_rot.shape[-1] ** -0.5)
     scores = jnp.where(seen_mask[:, :, None, None, :], scores, -1e30)
     probs_bf = jax.nn.softmax(scores, axis=-1).astype(BF16)
-    context = jnp.einsum('nbkgt,nbtkd->nbkgd', probs_bf, v_upd, preferred_element_type=F32).astype(BF16)
-    return context, k_upd, v_upd
-
-
-def mlp_partial(hidden, gain, gate_mat, up_mat, down_mat):
-    normed = rms_norm(hidden, gain)
-    gate_act = dot32(normed, gate_mat).astype(BF16)
-    up_proj = dot32(normed, up_mat).astype(BF16)
-    swi_act = (jax.nn.silu(gate_act.astype(F32)) * up_proj.astype(F32)).astype(BF16)
-    return dot32(swi_act, down_mat)
-
-
-def run_decode(tokens, hold, c_len, k_cache, v_cache, attn_gain, mlp_gain, qkv_dec, out_dec, gate_mat, up_mat, down_mat, tp_count):
+    return jnp.einsum('nbkgt,nbtkd->nbkgd', probs_bf, v_upd, preferred_element_type=F32).astype(BF16)
+
+
+def decode_attend(tokens, c_len, k_cache, v_cache, attn_gain, qkv_dec, out_dec, tp_count):
     group_size = qkv_dec.shape[2] - 2
     cos_tab, sin_tab = rope_tables(c_len, qkv_dec.shape[-1])
     cache_pos = jnp.arange(k_cache.shape[2])
@@ -332,13 +365,11 @@
     qkv_all = jnp.einsum('nse,ekcd->nskcd', normed, qkv_dec, preferred_element_type=F32).astype(BF16)
     q_rot = apply_rope(qkv_all[:, :, :, :group_size], cos_tab[:, :, None, None, :], sin_tab[:, :, None, None, :])
     k_rot = apply_rope(qkv_all[:, :, :, group_size], cos_tab[:, :, None, :], sin_tab[:, :, None, :])
-    context, k_upd, v_upd = decode_attention(q_rot, k_rot, qkv_all[:, :, :, group_size + 1], k_cache, v_cache, write_mask, seen_mask)
+    v_new = qkv_all[:, :, :, group_size + 1]
+    context = decode_attention(q_rot, k_rot, v_new, k_cache, v_cache, write_mask, seen_mask)
     attn_part = jnp.einsum('nskgd,kgde->nse', context, out_dec, preferred_element_type=F32)
     hidden = residual_add(tokens, small_sum(attn_part, tp_count).astype(BF16))
-    hidden = after(hidden, hold)
-    down_part = mlp_partial(hidden[0], mlp_gain, gate_mat, up_mat, down_mat)[None]
-    hidden = residual_add(hidden, small_sum(down_part, tp_count).astype(BF16))
-    return hidden, k_upd[None], v_upd[None]
+    return hidden, k_rot, v_new, write_mask
 
 
 def solution(mesh):
@@ -376,44 +407,62 @@
         sin_full = jnp.concatenate([-sin_tab, sin_tab], axis=-1)
         k_rot, pack = kv_prep(qkv, s_len, cos_full, sin_full, kv_local, group_size, head_dim)
 
-        rows = seq_len // CHUNKS
-        own_rows = rows // tp_count
         place = tp_index.astype(jnp.int32)[None]
-        contexts = [attend_chunk(qkv, k_rot, cos_full, sin_full, s_len, c, rows, kv_local, group_size, head_dim) for c in range(CHUNKS)]
+        edges = chunk_edges(seq_len)
+        spans = list(zip(edges[:-1], edges[1:]))
+        contexts = []
+        for start, stop in spans:
+            lengths = after(s_len, contexts[-1]) if contexts else s_len
+            contexts.append(attend_chunk(qkv, k_rot, cos_full, sin_full, lengths, start, stop - start, kv_local, group_size, head_dim))
         ctx_parts = [ring_gather(contexts[0], tp_count)]
         ctx_parts += [[lax.all_gather(context, 'tp', axis=0)] for context in contexts[1:]]
         partials, blocks, finals, hiddens, firsts = [], [], [], [], []
+        tok_part = None
 
         def finish(c):
-            summed = scatter_last(partials[c], blocks[c], tp_count, tp_index)
+            summed = scatter_last(partials[c][0], blocks[c], tp_count)
+            own_rows = summed.shape[0]
             own_hidden = lax.dynamic_slice_in_dim(hiddens[c], tp_index * own_rows, own_rows, axis=0)
             finals.append(residual_add(own_hidden, summed.astype(BF16)))
 
-        for chunk in range(CHUNKS):
+        for chunk, (start, stop) in enumerate(spans):
             deps = []
             if chunk >= 2:
                 finish(chunk - 2)
                 deps.append(finals[chunk - 2])
             if chunk >= 1:
-                deps.append(partials[chunk - 1])
+                deps.append(partials[chunk - 1][0])
             parts = ctx_parts[chunk]
             if deps:
                 parts = list(lax.optimization_barrier(tuple(parts) + tuple(deps))[:len(parts)])
-            hidden = project_chunk(parts, out_full, x, chunk, rows, place, tp_count)
+            hidden = project_chunk(parts, out_full, x, start, stop - start, place, tp_count)
             if chunk >= 1:
-                blocks.append(scatter_add(partials[chunk - 1], firsts[chunk - 1], tp_count, tp_index))
+                blocks.append(scatter_add(partials[chunk - 1], firsts[chunk - 1]))
                 hidden = after(hidden, *blocks[chunk - 1])
             hiddens.append(hidden)
-            partial = mlp_chunk(hidden, mlp_norm, gate_mat, up_mat, down_mat).reshape(tp_count, own_rows, width)
+            extra = None
+            if chunk == 2:
+                held = after(tokens, partials[0][0])
+                tok_hidden, k_row, v_row, write_mask = decode_attend(held, c_len, k_cache[0], v_cache[0], attn_norm[0], w_qkv_dec[0], w_out_dec[0], tp_count)
+                extra = tok_hidden[0]
+            partial = mlp_chunk(hidden, mlp_norm, gate_mat, up_mat, down_mat, place, tp_count, extra)
             partials.append(partial)
-            firsts.append(scatter_first(partial, tp_count, tp_index))
-        finish(CHUNKS - 2)
-        blocks.append(scatter_add(partials[-1], firsts[-1], tp_count, tp_index))
-        finish(CHUNKS - 1)
-        out = jnp.concatenate([lax.all_gather(final, 'tp', axis=0, tiled=True) for final in finals], axis=0)
-
-        k_prompt, v_prompt = hand_off(pack, tp_count, node_count, tp_index)
-        tok_out, k_new, v_new = run_decode(after(tokens, partials[CHUNKS - 1]), partials[CHUNKS - 1], c_len, k_cache[0], v_cache[0], attn_norm[0], mlp_norm[0], w_qkv_dec[0], w_out_dec[0], gate_mat, up_mat, down_mat, tp_count)
+            if chunk == 2:
+                tok_part = partial[5]
+            firsts.append(scatter_first(partial, tp_count))
+        finish(len(spans) - 2)
+        blocks.append(scatter_add(partials[-1], firsts[-1]))
+        finish(len(spans) - 1)
+        out = jnp.zeros((seq_len, width), BF16)
+        for final, (start, stop) in zip(finals, spans):
+            out = lax.dynamic_update_slice(out, lax.all_gather(final, 'tp', axis=0, tiled=True), (start, 0))
+
+        k_prompt, v_prompt = hand_off(after(pack, partials[0][0]), tp_count, node_count, tp_index)
+        tok_sum = small_sum(tok_part[None], tp_count)
+        tok_out = residual_add(tok_hidden, tok_sum.astype(BF16))
+        k_row, v_row = lax.optimization_barrier((k_row, v_row, partials[-1][0]))[:2]
+        k_new = write_cache(k_cache[0], k_row, write_mask)[None]
+        v_new = write_cache(v_cache[0], v_row, write_mask)[None]
         return out[None], tok_out, k_prompt, v_prompt, k_new, v_new
 
     return jax.shard_map(local_fn, mesh=mesh, in_specs=(row_spec, len_spec, row_spec, clen_spec, cache_spec, cache_spec, gain_spec, gain_spec, qkv_spec, out_spec, qkv_spec, out_spec, col_spec, col_spec, down_spec), out_specs=(row_spec, row_spec, prompt_kv_spec, prompt_kv_spec, cache_spec, cache_spec), check_vma=False)

time: 929 us -> 944 us (1.016)
  Pallas kernels: 398 us -> 434 us
  matrix products: 85.4 us -> 54 us
  local copies, waits for them, and re-layouts: 77.5 us -> 97.3 us
  other arithmetic: 95.6 us -> 80.5 us
    dot_general x3 -> x1, matrix products: 68.8 us -> 34.8 us  [dot32(): return jnp.dot(a, b, preferred_element_type=F32)]
    pallas_call x8 -> x10, Pallas kernels: 306 us -> 331 us  [the longest x5 265 us: mlp_chunk(): pl.pallas_call(functools.partial(mlp_kernel, tp_count=tp_count, extra=ext...]
    ppermute x12 -> x14, waiting for transfers between devices: 87.5 us -> 67.4 us  [make_ring(): lax.ppermute(x, 'tp', up)]
    dynamic_update_slice x0 -> x10, other arithmetic: none -> 18.8 us  [the longest x5 9.97 us: scatter_add(): up_block = lax.dynamic_update_slice(succ, succ[:half] + from_prev, (0, 0))]
    dynamic_update_slice x0 -> x4, local copies, waits for them, and re-layouts: none -> 17.2 us  [local_fn(): lax.dynamic_update_slice(out, lax.all_gather(final, 'tp', axis=0, tiled=T...]
    all_gather x4 -> x5, waiting for transfers between devices: 2.42 us -> 19.3 us  [local_fn(): lax.all_gather(final, 'tp', axis=0, tiled=True)]
    slice x6 -> x2, local copies, waits for them, and re-layouts: 13.6 us -> 0.04 us  [the longest x1 0.02 us: ring_gather(): far_a = send_up(prev[:half])]
    broadcast_in_dim x1 -> x0, other arithmetic: 13.6 us -> none  [local_fn(): return (out[None], tok_out, k_prompt, v_prompt, k_new, v_new)]
  transfers between devices with their start and end apart: 36 -> 42, of which waited for: 11 -> 13; matrix products, arithmetic and copies ran while one was open for 26% -> 22% of each run, Pallas kernels for 43% -> 47%
where the time goes in v2:
time: 944 us; the launch traced here: 931 us
  Pallas kernels  434 us (46%)
  waiting for transfers between devices  197 us (21%)
  local copies, waits for them, and re-layouts  97.3 us (10%)
  other arithmetic  80.5 us (9%)
  matrix products  54 us (6%)
  starting transfers between devices  52.5 us (6%)
  between operations  15.5 us (2%)
    pallas_call x5, Pallas kernels, mlp_chunk(): pl.pallas_call(functools.partial(mlp_kernel, tp_count=tp_count, extra=ext...  265 us
    ppermute x14, waiting for transfers between devices, make_ring(): lax.ppermute(x, 'tp', down)  110 us
    pallas_call x5, Pallas kernels, project_chunk(): pl.pallas_call(functools.partial(project_kernel, tp_count=tp_count, n_in=...  98.1 us
    unnamed x73, local copies, waits for them, and re-layouts  69.1 us
    ppermute x14, waiting for transfers between devices, make_ring(): lax.ppermute(x, 'tp', up)  67.4 us
    pallas_call x5, Pallas kernels, attend_chunk(): pl.pallas_call(functools.partial(attend_kernel, start=start, sub=sub, n_q...  65.9 us
    dot_general x1, matrix products, dot32(): return jnp.dot(a, b, preferred_element_type=F32)  34.8 us
    select_n x2, other arithmetic, write_cache(): return jnp.where(write_mask[:, :, :, None, None], new[:, :, None], old)  26.7 us
  transfers between devices with their start and end apart: 42, of which 13 were waited for; matrix products, arithmetic and copies ran while one was open for 22% of the time, Pallas kernels for 47%

profile of v2, /device:TPU:104, one launch (start us, length us, event | category | flops | bytes accessed | tf_op | source)
XLA Modules:
  0.0 930.9 jit_solution(6534163065780705167)
XLA Ops:
  11.1 31.1 %copy.29 = bf16[1,4096,2,6,128]{1,4,3,2,0:T(8,128)(2,1)} copy(bf16[1,4096,2,6,128]{4,2,3,1,0:T(2,128)(2,1)} %param.23) | data formatting | bytes 25165824 | tf_op args[8]
  55.2 34.8 %fusion.10.refs_0_.refs_1_.refs_2_.refs_3_.refs_4_.refs_7_ = bf16[2048,1536]{1,0:T(8,128)(2,1)} fusion(bf16[4096,1536]{0,1:T(8,128)(2,1)} %bitcast.113, bf16[1,2048,4096]{2,1,0:T(8,128)(2,1)} %param.15, f32[4096]{0:T(1024)S(1)} %bitcast.123, f32[2048]{0:T(1024)S(1)} %add_rsqrt_fusion), kind=kOutput, calls=%fused_computation.16 | convolution fusion | flops 25806503936 | bytes 35676160 | tf_op jit(solution)/shard_map/dot_general | solution.py:47
  95.0 11.7 %attend.6 = bf16[512,1024]{1,0:T(8,128)(2,1)} custom-call(s32[1]{0:T(128)S(6)} %copy.84.slen_ref, bf16[2048,1536]{1,0:T(8,128)(2,1)} %fusion.10.refs_0_.refs_1_.refs_2_.refs_3_.refs_4_.refs_7_, bf16[2048,1536]{1,0:T(8,128)(2,1)} %fusion.10.refs_0_.refs_1_.refs_2_.refs_3_.refs_4_.refs_7_, f32[2048,128]{1,0:T(8,128)} %get-tuple-element.124.refs_4_.refs_1_.refs_2_.refs_3_, ...), custom_call_target="tpu_custom_call" | custom-call | flops 4831838208 | bytes 2097152 | tf_op jit(solution)/shard_map/attend/pallas_call | solution.py:128
  107.0 15.3 %attend.7 = bf16[512,1024]{1,0:T(8,128)(2,1)} custom-call(s32[1]{0:T(128)S(6)} %copy.84.slen_ref, bf16[2048,1536]{1,0:T(8,128)(2,1)} %fusion.10.refs_0_.refs_1_.refs_2_.refs_3_.refs_4_.refs_7_, bf16[2048,1536]{1,0:T(8,128)(2,1)} %fusion.10.refs_0_.refs_1_.refs_2_.refs_3_.refs_4_.refs_7_, f32[2048,128]{1,0:T(8,128)} %get-tuple-element.124.refs_4_.refs_1_.refs_2_.refs_3_, ...), custom_call_target="tpu_custom_call" | custom-call | flops 8053063680 | bytes 2097152 | tf_op jit(solution)/shard_map/attend/pallas_call | solution.py:128
  122.5 19.1 %attend.8 = bf16[512,1024]{1,0:T(8,128)(2,1)} custom-call(s32[1]{0:T(128)S(6)} %copy.84.slen_ref, bf16[2048,1536]{1,0:T(8,128)(2,1)} %fusion.10.refs_0_.refs_1_.refs_2_.refs_3_.refs_4_.refs_7_, bf16[2048,1536]{1,0:T(8,128)(2,1)} %fusion.10.refs_0_.refs_1_.refs_2_.refs_3_.refs_4_.refs_7_, f32[2048,128]{1,0:T(8,128)} %get-tuple-element.124.refs_4_.refs_1_.refs_2_.refs_3_, ...), custom_call_target="tpu_custom_call" | custom-call | flops 11274289152 | bytes 2097152 | tf_op jit(solution)/shard_map/attend/pallas_call | solution.py:128
  152.1 12.3 %attend.9 = bf16[256,1024]{1,0:T(8,128)(2,1)} custom-call(s32[1]{0:T(128)S(6)} %copy.84.slen_ref, bf16[2048,1536]{1,0:T(8,128)(2,1)} %fusion.10.refs_0_.refs_1_.refs_2_.refs_3_.refs_4_.refs_7_, f32[2048,128]{1,0:T(8,128)} %get-tuple-element.124.refs_4_.refs_1_.refs_2_.refs_3_, f32[2048,128]{1,0:T(8,128)} %get-tuple-element.125.refs_5_.refs_2_.refs_4_, ...), custom_call_target="tpu_custom_call" | custom-call | flops 6442450944 | bytes 1048576 | tf_op jit(solution)/shard_map/attend/pallas_call | solution.py:128
  164.6 10.9 %collective-permute-done.1.refs_4_ = bf16[256,1024]{1,0:T(8,128)(2,1)S(1)} collective-permute-done((bf16[256,1024]{1,0:T(8,128)(2,1)}, bf16[256,1024]{1,0:T(8,128)(2,1)S(1)}, u32[]{:S(2)}, u32[]{:S(2)}) %collective-permute-start.1) | collective-permute-done | bytes 524320 | tf_op jit(solution)/shard_map/ppermute | solution.py:281
  185.6 16.6 %project.5.h_ref = bf16[256,4096]{1,0:T(8,128)(2,1)S(1)} custom-call(s32[1]{0:T(128)} %bitcast.place_ref, bf16[256,1024]{1,0:T(8,128)(2,1)S(1)} %copy-done.8, bf16[256,1024]{1,0:T(8,128)(2,1)S(1)} %collective-permute-done.refs_1_, bf16[128,1024]{1,0:T(8,128)(2,1)S(1)} %collective-permute-done.2.refs_2_, ...), custom_call_target="tpu_custom_call" | custom-call | flops 8589934592 | bytes 33554432 | tf_op jit(solution)/shard_map/project/pallas_call | solution.py:180
  203.5 38.9 %mlp.5 = (f32[64,4096]{1,0:T(8,128)}, f32[64,4096]{1,0:T(8,128)}, f32[32,4096]{1,0:T(8,128)}, f32[32,4096]{1,0:T(8,128)}, f32[64,4096]{1,0:T(8,128)}) custom-call(s32[1]{0:T(128)} %bitcast.place_ref, bf16[256,4096]{1,0:T(8,128)(2,1)} %copy-done, bf16[1,4096]{1,0:T(2,128)(2,1)} %gain_ref.9, bf16[4096,3584]{1,0:T(8,128)(2,1)} %bitcast.98, ...), custom_call_target="tpu_custom_call" | custom-call | flops 22548578304 | bytes 88080384 | tf_op jit(solution)/shard_map/mlp/pallas_call | solution.py:261
  251.8 12.7 %broadcast_select_fusion.3 = (bf16[16,512,2,128]{3,2,1,0:T(2,128)(2,1)}, bf16[16,512,2,128]{3,2,1,0:T(2,128)(2,1)}) fusion(pred[16,512]{1,0:T(8,128)(4,1)S(1)} %get-tuple-element.121, bf16[1,1,16,512,2,128]{5,4,3,2,1,0:T(2,128)(2,1)S(1)} %copy-done.10, bf16[16,2,128]{2,1,0:T(2,128)(2,1)S(1)} %copy.31, bf16[1,1,16,512,2,128]{5,4,3,2,1,0:T(2,128)(2,1)S(1)} %copy-done.11, ...), kind=kLoop, calls=%fused_computation.15 | loop fusion | flops 4194304 | bytes 16801792 | tf_op jit(solution)/shard_map/jit(_where)/select_n | solution.py:346
  288.0 21.7 %project.6.h_ref = bf16[512,4096]{1,0:T(8,128)(2,1)S(1)} custom-call(s32[1]{0:T(128)} %bitcast.place_ref, bf16[4,512,1024]{2,1,0:T(8,128)(2,1)S(1)} %bitcast.88, bf16[4096,4096]{1,0:T(8,128)(2,1)} %all-gather.15.cloned.1.call-done.refs_5_.refs_1_, bf16[2048,4096]{1,0:T(8,128)(2,1)} %bitcast.91, bf16[2048,4096]{1,0:T(8,128)(2,1)} %bitcast.92), custom_call_target="tpu_custom_call" | custom-call | flops 17179869184 | bytes 33554432 | tf_op jit(solution)/shard_map/project/pallas_call | solution.py:180
  323.2 61.1 %mlp.6 = (f32[128,4096]{1,0:T(8,128)}, f32[128,4096]{1,0:T(8,128)}, f32[64,4096]{1,0:T(8,128)}, f32[64,4096]{1,0:T(8,128)}, f32[128,4096]{1,0:T(8,128)}) custom-call(s32[1]{0:T(128)} %bitcast.place_ref, bf16[512,4096]{1,0:T(8,128)(2,1)} %copy-done.2, bf16[1,4096]{1,0:T(2,128)(2,1)} %gain_ref.9, bf16[4096,3584]{1,0:T(8,128)(2,1)} %bitcast.99, ...), custom_call_target="tpu_custom_call" | custom-call | flops 45097156608 | bytes 88080384 | tf_op jit(solution)/shard_map/mlp/pallas_call | solution.py:261
  391.1 21.8 %project.7.h_ref = bf16[512,4096]{1,0:T(8,128)(2,1)S(1)} custom-call(s32[1]{0:T(128)} %bitcast.place_ref, bf16[4,512,1024]{2,1,0:T(8,128)(2,1)S(1)} %bitcast.87, bf16[4096,4096]{1,0:T(8,128)(2,1)} %all-gather.15.cloned.1.call-done.refs_5_.refs_1_, bf16[2048,4096]{1,0:T(8,128)(2,1)} %bitcast.93, bf16[2048,4096]{1,0:T(8,128)(2,1)} %bitcast.94), custom_call_target="tpu_custom_call" | custom-call | flops 17179869184 | bytes 33554432 | tf_op jit(solution)/shard_map/project/pallas_call | solution.py:180
  419.0 64.2 %mlp.7 = (f32[128,4096]{1,0:T(8,128)}, f32[128,4096]{1,0:T(8,128)}, f32[64,4096]{1,0:T(8,128)}, f32[64,4096]{1,0:T(8,128)}, f32[128,4096]{1,0:T(8,128)}, /*index=5*/f32[16,4096]{1,0:T(8,128)}) custom-call(s32[1]{0:T(128)} %bitcast.place_ref, bf16[512,4096]{1,0:T(8,128)(2,1)} %copy-done.3, bf16[1,4096]{1,0:T(2,128)(2,1)} %gain_ref.9, ...), custom_call_target="tpu_custom_call" | custom-call | flops 45097156608 | bytes 88080384 | tf_op jit(solution)/shard_map/mlp/pallas_call | solution.py:261
  495.8 53.2 %collective-permute-done.17 = f32[64,4096]{1,0:T(8,128)S(1)} collective-permute-done((f32[64,4096]{1,0:T(8,128)}, f32[64,4096]{1,0:T(8,128)S(1)}, u32[]{:S(2)}, u32[]{:S(2)}) %collective-permute-start.17) | collective-permute-done | bytes 1048608 | tf_op jit(solution)/shard_map/ppermute | solution.py:281
  551.4 40.3 %collective-permute-done.15 = f32[64,4096]{1,0:T(8,128)S(1)} collective-permute-done((f32[64,4096]{1,0:T(8,128)}, f32[64,4096]{1,0:T(8,128)S(1)}, u32[]{:S(2)}, u32[]{:S(2)}) %collective-permute-start.15) | collective-permute-done | bytes 1048608 | tf_op jit(solution)/shard_map/ppermute | solution.py:281
  602.6 21.9 %project.8.h_ref = bf16[512,4096]{1,0:T(8,128)(2,1)S(1)} custom-call(s32[1]{0:T(128)} %bitcast.place_ref, bf16[4,512,1024]{2,1,0:T(8,128)(2,1)S(1)} %bitcast.86, bf16[4096,4096]{1,0:T(8,128)(2,1)} %all-gather.15.cloned.1.call-done.refs_5_.refs_1_, bf16[2048,4096]{1,0:T(8,128)(2,1)} %bitcast.95, bf16[2048,4096]{1,0:T(8,128)(2,1)} %bitcast.96), custom_call_target="tpu_custom_call" | custom-call | flops 17179869184 | bytes 33554432 | tf_op jit(solution)/shard_map/project/pallas_call | solution.py:180
  626.6 61.4 %mlp.8 = (f32[128,4096]{1,0:T(8,128)}, f32[128,4096]{1,0:T(8,128)}, f32[64,4096]{1,0:T(8,128)}, f32[64,4096]{1,0:T(8,128)}, f32[128,4096]{1,0:T(8,128)}) custom-call(s32[1]{0:T(128)} %bitcast.place_ref, bf16[512,4096]{1,0:T(8,128)(2,1)} %copy-done.4, bf16[1,4096]{1,0:T(2,128)(2,1)} %gain_ref.9, bf16[4096,3584]{1,0:T(8,128)(2,1)} %bitcast.101, ...), custom_call_target="tpu_custom_call" | custom-call | flops 45097156608 | bytes 88080384 | tf_op jit(solution)/shard_map/mlp/pallas_call | solution.py:261
  702.2 25.5 %collective-permute-done.21 = f32[64,4096]{1,0:T(8,128)S(1)} collective-permute-done((f32[64,4096]{1,0:T(8,128)}, f32[64,4096]{1,0:T(8,128)S(1)}, u32[]{:S(2)}, u32[]{:S(2)}) %collective-permute-start.21) | collective-permute-done | bytes 1048608 | tf_op jit(solution)/shard_map/ppermute | solution.py:281
  763.8 16.1 %project.9.h_ref = bf16[256,4096]{1,0:T(8,128)(2,1)S(1)} custom-call(s32[1]{0:T(128)} %bitcast.place_ref, bf16[4,256,1024]{2,1,0:T(8,128)(2,1)S(1)} %bitcast.89, bf16[4096,4096]{1,0:T(8,128)(2,1)} %all-gather.15.cloned.1.call-done.refs_5_.refs_1_, bf16[2048,4096]{1,0:T(8,128)(2,1)} %bitcast.97), custom_call_target="tpu_custom_call" | custom-call | flops 8589934592 | bytes 33554432 | tf_op jit(solution)/shard_map/project/pallas_call | solution.py:180
  781.2 10.3 %collective-permute-done.22 = f32[128,4096]{1,0:T(8,128)S(1)} collective-permute-done((f32[128,4096]{1,0:T(8,128)}, f32[128,4096]{1,0:T(8,128)S(1)}, u32[]{:S(2)}, u32[]{:S(2)}) %collective-permute-start.22) | collective-permute-done | bytes 2097184 | tf_op jit(solution)/shard_map/ppermute | solution.py:281
  800.6 39.5 %mlp.9 = (f32[64,4096]{1,0:T(8,128)}, f32[64,4096]{1,0:T(8,128)}, f32[32,4096]{1,0:T(8,128)}, f32[32,4096]{1,0:T(8,128)}, f32[64,4096]{1,0:T(8,128)}) custom-call(s32[1]{0:T(128)} %bitcast.place_ref, bf16[256,4096]{1,0:T(8,128)(2,1)} %copy-done.1, bf16[1,4096]{1,0:T(2,128)(2,1)} %gain_ref.9, bf16[4096,3584]{1,0:T(8,128)(2,1)} %bitcast.102, ...), custom_call_target="tpu_custom_call" | custom-call | flops 22548578304 | bytes 88080384 | tf_op jit(solution)/shard_map/mlp/pallas_call | solution.py:261
  842.5 14.0 %broadcast_select_fusion = (bf16[1,1,16,512,2,128]{5,4,3,2,1,0:T(2,128)(2,1)}, bf16[1,1,16,512,2,128]{5,4,3,2,1,0:T(2,128)(2,1)}) fusion(bf16[1,1,16,512,2,128]{5,4,3,2,1,0:T(2,128)(2,1)} %param.20, pred[16,512]{1,0:T(8,128)(4,1)S(1)} %copy-done.26, bf16[16,2,128]{2,1,0:T(2,128)(2,1)S(1)} %copy.37, bf16[1,1,16,512,2,128]{5,4,3,2,1,0:T(2,128)(2,1)} %param.19, ...), kind=kLoop, calls=%fused_computation.12 | loop fusion | flops 4194304 | bytes 16801792 | tf_op jit(solution)/shard_map/jit(_where)/select_n | solution.py:346
  901.5 19.3 %all-gather.25.cloned.1.call-done = bf16[256,4096]{1,0:T(8,128)(2,1)} async-done(((bf16[64,4096]{1,0:T(8,128)(2,1)}), bf16[256,4096]{1,0:T(8,128)(2,1)}) %all-gather.25.cloned.1.call-update) | async-done | bytes 2097168 | tf_op jit(solution)/shard_map/all_gather | solution.py:458
  (217 shorter events, 241.7 us)
Async XLA Ops:
  7.2 178.5 %all-gather.15.cloned.1.call-start = ((), (), s32[]{:S(2)}) async-start(), calls=%async_computation | async-start | bytes 34603008 | tf_op jit(solution)/shard_map/all_gather | solution.py:401
  9.6 273.8 %all-gather.27.cloned.1.call-start = ((), (), s32[]{:S(2)}) async-start(), calls=%async_computation.6 | async-start | bytes 5242880 | tf_op jit(solution)/shard_map/all_gather | solution.py:418
  106.8 282.1 %all-gather.29.cloned.1.call-start = ((), (), s32[]{:S(2)}) async-start(), calls=%async_computation.7 | async-start | bytes 5242880 | tf_op jit(solution)/shard_map/all_gather | solution.py:418
  122.4 478.0 %all-gather.31.cloned.1.call-start = ((), (), s32[]{:S(2)}) async-start(), calls=%async_computation.8 | async-start | bytes 5242880 | tf_op jit(solution)/shard_map/all_gather | solution.py:418
  141.7 620.5 %all-gather.33.cloned.1.call-start = ((), (), s32[]{:S(2)}) async-start(), calls=%async_computation.9 | async-start | bytes 2621440 | tf_op jit(solution)/shard_map/all_gather | solution.py:418
  164.5 705.9 %all-gather.17.cloned.1.call-start = ((), (), s32[]{:S(2)}) async-start(), calls=%async_computation.1 | async-start | bytes 2621440 | tf_op jit(solution)/shard_map/all_gather | solution.py:458
  318.3 68.2 %collective-permute-start.7 = (f32[64,4096]{1,0:T(8,128)}, f32[64,4096]{1,0:T(8,128)S(1)}, u32[]{:S(2)}, u32[]{:S(2)}) collective-permute-start(f32[64,4096]{1,0:T(8,128)} %add_dynamic-update-slice_fusion.8), channel_id=1, source_target_pairs={{8,0},{16,8},{24,16},{0,24},{9,1},{17,9},{25,17},{1,25},{10,2},{18... | collective-permute-start | bytes 3145736 | tf_op jit(solution)/shard_map/ppermute | solution.py:281
  322.8 63.8 %collective-permute-start.5 = (f32[64,4096]{1,0:T(8,128)}, f32[64,4096]{1,0:T(8,128)}, u32[]{:S(2)}, u32[]{:S(2)}) collective-permute-start(f32[64,4096]{1,0:T(8,128)} %add_dynamic-update-slice_fusion.9), channel_id=1, source_target_pairs={{0,8},{8,16},{16,24},{24,0},{1,9},{9,17},{17,25},{25,1},{2,10},{10... | collective-permute-start | bytes 3145736 | tf_op jit(solution)/shard_map/ppermute | solution.py:281
  483.2 65.8 %collective-permute-start.17 = (f32[64,4096]{1,0:T(8,128)}, f32[64,4096]{1,0:T(8,128)S(1)}, u32[]{:S(2)}, u32[]{:S(2)}) collective-permute-start(f32[64,4096]{1,0:T(8,128)} %get-tuple-element.72), channel_id=1, source_target_pairs={{8,0},{16,8},{24,16},{0,24},{9,1},{17,9},{25,17},{1,25},{10,2},{18... | collective-permute-start | bytes 3145736 | tf_op jit(solution)/shard_map/ppermute | solution.py:281
  486.0 109.7 %collective-permute-start.11 = (f32[128,4096]{1,0:T(8,128)}, f32[128,4096]{1,0:T(8,128)}, u32[]{:S(2)}, u32[]{:S(2)}) collective-permute-start(f32[128,4096]{1,0:T(8,128)} %copy-done.19), channel_id=1, source_target_pairs={{8,0},{16,8},{24,16},{0,24},{9,1},{17,9},{25,17},{1,25},{10,2},{18... | collective-permute-start | bytes 6291464 | tf_op jit(solution)/shard_map/ppermute | solution.py:281
  488.1 108.0 %collective-permute-start.9 = (f32[128,4096]{1,0:T(8,128)}, f32[128,4096]{1,0:T(8,128)}, u32[]{:S(2)}, u32[]{:S(2)}) collective-permute-start(f32[128,4096]{1,0:T(8,128)} %copy-done.21), channel_id=1, source_target_pairs={{0,8},{8,16},{16,24},{24,0},{1,9},{9,17},{17,25},{25,1},{2,10},{10... | collective-permute-start | bytes 6291464 | tf_op jit(solution)/shard_map/ppermute | solution.py:281
  488.1 399.2 %all-gather.19.cloned.1.call-start = ((), (), s32[]{:S(2)}) async-start(), calls=%async_computation.2 | async-start | bytes 5242880 | tf_op jit(solution)/shard_map/all_gather | solution.py:458
  488.2 103.5 %collective-permute-start.15 = (f32[64,4096]{1,0:T(8,128)}, f32[64,4096]{1,0:T(8,128)S(1)}, u32[]{:S(2)}, u32[]{:S(2)}) collective-permute-start(f32[64,4096]{1,0:T(8,128)} %get-tuple-element.70), channel_id=1, source_target_pairs={{0,8},{8,16},{16,24},{24,0},{1,9},{9,17},{17,25},{25,1},{2,10},{10... | collective-permute-start | bytes 3145736 | tf_op jit(solution)/shard_map/ppermute | solution.py:281
  489.8 204.6 %collective-permute-start.30 = (bf16[2,2048,128]{2,1,0:T(8,128)(2,1)}, bf16[2,2048,128]{2,1,0:T(8,128)(2,1)}, u32[]{:S(2)}, u32[]{:S(2)}) collective-permute-start(bf16[2,2048,128]{2,1,0:T(8,128)(2,1)} %get-tuple-element.102), channel_id=1, source_target_pairs={{0,4},{8,20},{16,12},{24,28},{1,5},{9,21},{17,13},{25,29},{2,6},{1... | collective-permute-start | bytes 3145736 | tf_op jit(solution)/shard_map/ppermute | solution.py:338
  549.0 145.4 %collective-permute-start.31 = (bf16[2,2048,128]{2,1,0:T(8,128)(2,1)}, bf16[2,2048,128]{2,1,0:T(8,128)(2,1)}, u32[]{:S(2)}, u32[]{:S(2)}) collective-permute-start(bf16[2,2048,128]{2,1,0:T(8,128)(2,1)} %get-tuple-element.103), channel_id=1, source_target_pairs={{0,12},{8,28},{16,4},{24,20},{1,13},{9,29},{17,5},{25,21},{2,14},{... | collective-permute-start | bytes 3145736 | tf_op jit(solution)/shard_map/ppermute | solution.py:338
  591.7 98.1 %collective-permute-start.18 = (f32[128,4096]{1,0:T(8,128)}, f32[128,4096]{1,0:T(8,128)}, u32[]{:S(2)}, u32[]{:S(2)}) collective-permute-start(f32[128,4096]{1,0:T(8,128)} %add_dynamic-update-slice_fusion.2), channel_id=1, source_target_pairs={{8,0},{16,8},{24,16},{0,24},{9,1},{17,9},{25,17},{1,25},{10,2},{18... | collective-permute-start | bytes 6291464 | tf_op jit(solution)/shard_map/ppermute | solution.py:281
  595.8 94.0 %collective-permute-start.16 = (f32[128,4096]{1,0:T(8,128)}, f32[128,4096]{1,0:T(8,128)}, u32[]{:S(2)}, u32[]{:S(2)}) collective-permute-start(f32[128,4096]{1,0:T(8,128)} %add_dynamic-update-slice_fusion.3), channel_id=1, source_target_pairs={{0,8},{8,16},{16,24},{24,0},{1,9},{9,17},{17,25},{25,1},{2,10},{10... | collective-permute-start | bytes 6291464 | tf_op jit(solution)/shard_map/ppermute | solution.py:281
  600.1 291.9 %all-gather.21.cloned.1.call-start = ((), (), s32[]{:S(2)}) async-start(), calls=%async_computation.3 | async-start | bytes 5242880 | tf_op jit(solution)/shard_map/all_gather | solution.py:458
  693.9 202.9 %all-gather.23.cloned.1.call-start = ((), (), s32[]{:S(2)}) async-start(), calls=%async_computation.4 | async-start | bytes 5242880 | tf_op jit(solution)/shard_map/all_gather | solution.py:458
  697.0 64.4 %collective-permute-start.28 = (f32[1,16,4096]{2,1,0:T(8,128)S(1)}, f32[1,16,4096]{2,1,0:T(8,128)S(1)}, u32[]{:S(2)}, u32[]{:S(2)}) collective-permute-start(f32[1,16,4096]{2,1,0:T(8,128)S(1)} %bitcast.115), channel_id=1, source_target_pairs={{0,8},{8,16},{16,24},{24,0},{1,9},{9,17},{17,25},{25,1},{2,10},{10... | collective-permute-start | bytes 786440 | tf_op jit(solution)/shard_map/ppermute | solution.py:281
  697.6 63.9 %collective-permute-start.29 = (f32[1,16,4096]{2,1,0:T(8,128)S(1)}, f32[1,16,4096]{2,1,0:T(8,128)S(1)}, u32[]{:S(2)}, u32[]{:S(2)}) collective-permute-start(f32[1,16,4096]{2,1,0:T(8,128)S(1)} %bitcast.116), channel_id=1, source_target_pairs={{8,0},{16,8},{24,16},{0,24},{9,1},{17,9},{25,17},{1,25},{10,2},{18... | collective-permute-start | bytes 786440 | tf_op jit(solution)/shard_map/ppermute | solution.py:281
  699.1 62.3 %collective-permute-start.27 = (f32[1,16,4096]{2,1,0:T(8,128)S(1)}, f32[1,16,4096]{2,1,0:T(8,128)S(1)}, u32[]{:S(2)}, u32[]{:S(2)}) collective-permute-start(f32[1,16,4096]{2,1,0:T(8,128)S(1)} %bitcast.117), channel_id=1, source_target_pairs={{0,16},{8,24},{16,0},{24,8},{1,17},{9,25},{17,1},{25,9},{2,18},{10... | collective-permute-start | bytes 786440 | tf_op jit(solution)/shard_map/ppermute | solution.py:319
  730.0 61.5 %collective-permute-start.22 = (f32[128,4096]{1,0:T(8,128)}, f32[128,4096]{1,0:T(8,128)S(1)}, u32[]{:S(2)}, u32[]{:S(2)}) collective-permute-start(f32[128,4096]{1,0:T(8,128)} %add_dynamic-update-slice_fusion), channel_id=1, source_target_pairs={{8,0},{16,8},{24,16},{0,24},{9,1},{17,9},{25,17},{1,25},{10,2},{18... | collective-permute-start | bytes 6291464 | tf_op jit(solution)/shard_map/ppermute | solution.py:281
  800.4 120.3 %all-gather.25.cloned.1.call-start = ((), (), s32[]{:S(2)}) async-start(), calls=%async_computation.5 | async-start | bytes 2621440 | tf_op jit(solution)/shard_map/all_gather | solution.py:458
  (53 other events, 1314.4 us)
Sparse Core Ops, SparseCore 0:
  10.7 110.2 all-gather.14
  122.5 56.3 all-gather.26
  180.5 45.8 all-gather.28
  227.8 45.9 all-gather.30
  275.3 42.4 all-gather.32
  488.3 60.9 all-gather.16
  600.3 67.4 all-gather.18
  694.0 81.4 all-gather.20
  800.5 64.5 all-gather.22
  887.5 33.2 all-gather.24

commit v3 on v2

--- a/solution.py
+++ b/solution.py
@@ -9,14 +9,13 @@
 
 NORM_EPS = 1e-5
 ROPE_BASE = 10000.0
-EDGE_ROWS = 256
-MID_ROWS = 512
+CHUNK_ROWS = 512
 F32 = jnp.float32
 BF16 = jnp.bfloat16
 
 
 def chunk_edges(seq_len):
-    return [0] + list(range(EDGE_ROWS, seq_len, MID_ROWS)) + [seq_len]
+    return list(range(0, seq_len + 1, CHUNK_ROWS))
 
 
 def rope_tables(positions, head_dim):

time: 944 us -> 926 us (0.981)
  Pallas kernels: 434 us -> 403 us
  starting transfers between devices: 52.5 us -> 65.5 us
    ppermute x2, waiting for transfers between devices: 0.01 us -> 34.5 us  [hand_off(): got.append(lax.ppermute(piece, ('tp', 'node'), pairs))]
    all_gather x5 -> x4, waiting for transfers between devices: 19.3 us -> 0.01 us  [local_fn(): lax.all_gather(final, 'tp', axis=0, tiled=True)]
    pallas_call x5 -> x4, Pallas kernels: 265 us -> 249 us  [mlp_chunk(): pl.pallas_call(functools.partial(mlp_kernel, tp_count=tp_count, extra=ext...]
    ppermute x14 -> x12, waiting for transfers between devices: 110 us -> 95.1 us  [make_ring(): lax.ppermute(x, 'tp', down)]
    all_gather x4 -> x3, starting transfers between devices: 0.44 us -> 12 us  [local_fn(): lax.all_gather(context, 'tp', axis=0)]
    pallas_call x5 -> x4, Pallas kernels: 98.1 us -> 87.5 us  [project_chunk(): pl.pallas_call(functools.partial(project_kernel, tp_count=tp_count, n_in=...]
    ppermute x14 -> x12, waiting for transfers between devices: 67.4 us -> 75.3 us  [make_ring(): lax.ppermute(x, 'tp', up)]
    ppermute x14 -> x12, starting transfers between devices: 23.5 us -> 31.4 us  [make_ring(): lax.ppermute(x, 'tp', down)]
  transfers between devices with their start and end apart: 42 -> 36, of which waited for: 13 -> 16; matrix products, arithmetic and copies ran while one was open for 22% -> 22% of each run, Pallas kernels for 47% -> 44%
where the time goes in v3:
time: 926 us; the launch traced here: 913 us
  Pallas kernels  403 us (44%)
  waiting for transfers between devices  205 us (22%)
  local copies, waits for them, and re-layouts  90.3 us (10%)
  other arithmetic  79.4 us (9%)
  starting transfers between devices  65.5 us (7%)
  matrix products  53.9 us (6%)
  between operations  15.3 us (2%)
    pallas_call x4, Pallas kernels, mlp_chunk(): pl.pallas_call(functools.partial(mlp_kernel, tp_count=tp_count, extra=ext...  249 us
    ppermute x12, waiting for transfers between devices, make_ring(): lax.ppermute(x, 'tp', down)  95.1 us
    pallas_call x4, Pallas kernels, project_chunk(): pl.pallas_call(functools.partial(project_kernel, tp_count=tp_count, n_in=...  87.5 us
    ppermute x12, waiting for transfers between devices, make_ring(): lax.ppermute(x, 'tp', up)  75.3 us
    unnamed x61, local copies, waits for them, and re-layouts  63.5 us
    pallas_call x4, Pallas kernels, attend_chunk(): pl.pallas_call(functools.partial(attend_kernel, start=start, sub=sub, n_q...  62 us
    dot_general x1, matrix products, dot32(): return jnp.dot(a, b, preferred_element_type=F32)  34.8 us
    ppermute x2, waiting for transfers between devices, hand_off(): got.append(lax.ppermute(piece, ('tp', 'node'), pairs))  34.5 us
  transfers between devices with their start and end apart: 36, of which 16 were waited for; matrix products, arithmetic and copies ran while one was open for 22% of the time, Pallas kernels for 44%

profile of v3, /device:TPU:104, one launch (start us, length us, event | category | flops | bytes accessed | tf_op | source)
XLA Modules:
  0.0 912.9 jit_solution(18032766810835403433)
XLA Ops:
  11.1 31.2 %copy.29 = bf16[1,4096,2,6,128]{1,4,3,2,0:T(8,128)(2,1)} copy(bf16[1,4096,2,6,128]{4,2,3,1,0:T(2,128)(2,1)} %param.23) | data formatting | bytes 25165824 | tf_op args[8]
  56.0 34.8 %fusion.10.refs_0_.refs_1_.refs_2_.refs_3_.refs_7_ = bf16[2048,1536]{1,0:T(8,128)(2,1)} fusion(bf16[4096,1536]{0,1:T(8,128)(2,1)} %bitcast.94, bf16[1,2048,4096]{2,1,0:T(8,128)(2,1)} %param.15, f32[4096]{0:T(1024)S(1)} %bitcast.106, f32[2048]{0:T(1024)S(1)} %add_rsqrt_fusion), kind=kOutput, calls=%fused_computation.16 | convolution fusion | flops 25806503936 | bytes 35676160 | tf_op jit(solution)/shard_map/dot_general | solution.py:46
  95.9 13.3 %attend.5 = bf16[512,1024]{1,0:T(8,128)(2,1)} custom-call(s32[1]{0:T(128)S(6)} %copy.81.slen_ref, bf16[2048,1536]{1,0:T(8,128)(2,1)} %fusion.10.refs_0_.refs_1_.refs_2_.refs_3_.refs_7_, bf16[2048,1536]{1,0:T(8,128)(2,1)} %fusion.10.refs_0_.refs_1_.refs_2_.refs_3_.refs_7_, f32[2048,128]{1,0:T(8,128)} %get-tuple-element.108.refs_4_.refs_2_.refs_3_, ...), custom_call_target="tpu_custom_call" | custom-call | flops 6442450944 | bytes 2097152 | tf_op jit(solution)/shard_map/attend/pallas_call | solution.py:127
  121.2 17.2 %attend.6 = bf16[512,1024]{1,0:T(8,128)(2,1)} custom-call(s32[1]{0:T(128)S(6)} %copy.81.slen_ref, bf16[2048,1536]{1,0:T(8,128)(2,1)} %fusion.10.refs_0_.refs_1_.refs_2_.refs_3_.refs_7_, bf16[2048,1536]{1,0:T(8,128)(2,1)} %fusion.10.refs_0_.refs_1_.refs_2_.refs_3_.refs_7_, f32[2048,128]{1,0:T(8,128)} %get-tuple-element.108.refs_4_.refs_2_.refs_3_, ...), custom_call_target="tpu_custom_call" | custom-call | flops 9663676416 | bytes 2097152 | tf_op jit(solution)/shard_map/attend/pallas_call | solution.py:127
  151.8 20.7 %attend.7 = bf16[512,1024]{1,0:T(8,128)(2,1)} custom-call(s32[1]{0:T(128)S(6)} %copy.81.slen_ref, bf16[2048,1536]{1,0:T(8,128)(2,1)} %fusion.10.refs_0_.refs_1_.refs_2_.refs_3_.refs_7_, bf16[2048,1536]{1,0:T(8,128)(2,1)} %fusion.10.refs_0_.refs_1_.refs_2_.refs_3_.refs_7_, f32[2048,128]{1,0:T(8,128)} %get-tuple-element.108.refs_4_.refs_2_.refs_3_, ...), custom_call_target="tpu_custom_call" | custom-call | flops 12884901888 | bytes 2097152 | tf_op jit(solution)/shard_map/attend/pallas_call | solution.py:127
  172.6 15.4 %collective-permute-done.1.refs_4_ = bf16[512,1024]{1,0:T(8,128)(2,1)S(1)} collective-permute-done((bf16[512,1024]{1,0:T(8,128)(2,1)}, bf16[512,1024]{1,0:T(8,128)(2,1)S(1)}, u32[]{:S(2)}, u32[]{:S(2)}) %collective-permute-start.1) | collective-permute-done | bytes 1048608 | tf_op jit(solution)/shard_map/ppermute | solution.py:280
  192.9 23.0 %collective-permute-done.2.refs_2_ = bf16[256,1024]{1,0:T(8,128)(2,1)} collective-permute-done((bf16[256,1024]{1,0:T(8,128)(2,1)}, bf16[256,1024]{1,0:T(8,128)(2,1)}, u32[]{:S(2)}, u32[]{:S(2)}) %collective-permute-start.2) | collective-permute-done | bytes 524320 | tf_op jit(solution)/shard_map/ppermute | solution.py:280
  217.2 22.2 %project.4.h_ref = bf16[512,4096]{1,0:T(8,128)(2,1)S(1)} custom-call(s32[1]{0:T(128)} %bitcast.place_ref, bf16[512,1024]{1,0:T(8,128)(2,1)S(1)} %copy-done.4, bf16[512,1024]{1,0:T(8,128)(2,1)S(1)} %collective-permute-done.refs_1_, bf16[256,1024]{1,0:T(8,128)(2,1)} %collective-permute-done.2.refs_2_, bf16[256,1024]{1,0:T(8,128)(2,1)} %collective-permute-done.3.refs_3_, ...), custom_call_target="tpu_custom_call" | custom-call | flops 17179869184 | bytes 33554432 | tf_op jit(solution)/shard_map/project/pallas_call | solution.py:179
  241.4 61.7 %mlp.4 = (f32[128,4096]{1,0:T(8,128)}, f32[128,4096]{1,0:T(8,128)}, f32[64,4096]{1,0:T(8,128)}, f32[64,4096]{1,0:T(8,128)}, f32[128,4096]{1,0:T(8,128)}) custom-call(s32[1]{0:T(128)} %bitcast.place_ref, bf16[512,4096]{1,0:T(8,128)(2,1)} %copy-done.2, bf16[1,4096]{1,0:T(2,128)(2,1)} %gain_ref.7, bf16[4096,3584]{1,0:T(8,128)(2,1)} %bitcast.109, ...), custom_call_target="tpu_custom_call" | custom-call | flops 45097156608 | bytes 88080384 | tf_op jit(solution)/shard_map/mlp/pallas_call | solution.py:260
  315.5 12.7 %broadcast_select_fusion.3 = (bf16[16,512,2,128]{3,2,1,0:T(2,128)(2,1)}, bf16[16,512,2,128]{3,2,1,0:T(2,128)(2,1)}) fusion(pred[16,512]{1,0:T(8,128)(4,1)S(1)} %get-tuple-element.105, bf16[1,1,16,512,2,128]{5,4,3,2,1,0:T(2,128)(2,1)S(1)} %copy-done.8, bf16[16,2,128]{2,1,0:T(2,128)(2,1)S(1)} %copy.31, bf16[1,1,16,512,2,128]{5,4,3,2,1,0:T(2,128)(2,1)S(1)} %copy-done.10, ...), kind=kLoop, calls=%fused_computation.15 | loop fusion | flops 4194304 | bytes 16801792 | tf_op jit(solution)/shard_map/jit(_where)/select_n | solution.py:345
  328.2 21.7 %project.5.h_ref = bf16[512,4096]{1,0:T(8,128)(2,1)S(1)} custom-call(s32[1]{0:T(128)} %bitcast.place_ref, bf16[4,512,1024]{2,1,0:T(8,128)(2,1)S(1)} %bitcast.85, bf16[4096,4096]{1,0:T(8,128)(2,1)} %all-gather.12.cloned.1.call-done.refs_5_.refs_1_, bf16[2048,4096]{1,0:T(8,128)(2,1)} %bitcast.88, bf16[2048,4096]{1,0:T(8,128)(2,1)} %bitcast.89), custom_call_target="tpu_custom_call" | custom-call | flops 17179869184 | bytes 33554432 | tf_op jit(solution)/shard_map/project/pallas_call | solution.py:179
  364.1 61.3 %mlp.5 = (f32[128,4096]{1,0:T(8,128)}, f32[128,4096]{1,0:T(8,128)}, f32[64,4096]{1,0:T(8,128)}, f32[64,4096]{1,0:T(8,128)}, f32[128,4096]{1,0:T(8,128)}) custom-call(s32[1]{0:T(128)} %bitcast.place_ref, bf16[512,4096]{1,0:T(8,128)(2,1)} %copy-done.1, bf16[1,4096]{1,0:T(2,128)(2,1)} %gain_ref.7, bf16[4096,3584]{1,0:T(8,128)(2,1)} %bitcast.110, ...), custom_call_target="tpu_custom_call" | custom-call | flops 45097156608 | bytes 88080384 | tf_op jit(solution)/shard_map/mlp/pallas_call | solution.py:260
  448.3 12.0 %collective-permute-done.10 = f32[64,4096]{1,0:T(8,128)S(1)} collective-permute-done((f32[64,4096]{1,0:T(8,128)}, f32[64,4096]{1,0:T(8,128)S(1)}, u32[]{:S(2)}, u32[]{:S(2)}) %collective-permute-start.10) | collective-permute-done | bytes 1048608 | tf_op jit(solution)/shard_map/ppermute | solution.py:280
  469.8 12.0 %collective-permute-done.8 = f32[64,4096]{1,0:T(8,128)S(1)} collective-permute-done((f32[64,4096]{1,0:T(8,128)}, f32[64,4096]{1,0:T(8,128)S(1)}, u32[]{:S(2)}, u32[]{:S(2)}) %collective-permute-start.8) | collective-permute-done | bytes 1048608 | tf_op jit(solution)/shard_map/ppermute | solution.py:280
  496.0 21.8 %project.6.h_ref = bf16[512,4096]{1,0:T(8,128)(2,1)S(1)} custom-call(s32[1]{0:T(128)} %bitcast.place_ref, bf16[4,512,1024]{2,1,0:T(8,128)(2,1)S(1)} %bitcast.84, bf16[4096,4096]{1,0:T(8,128)(2,1)} %all-gather.12.cloned.1.call-done.refs_5_.refs_1_, bf16[2048,4096]{1,0:T(8,128)(2,1)} %bitcast.90, bf16[2048,4096]{1,0:T(8,128)(2,1)} %bitcast.91), custom_call_target="tpu_custom_call" | custom-call | flops 17179869184 | bytes 33554432 | tf_op jit(solution)/shard_map/project/pallas_call | solution.py:179
  519.8 18.6 %collective-permute-done.11 = f32[128,4096]{1,0:T(8,128)S(1)} collective-permute-done((f32[128,4096]{1,0:T(8,128)}, f32[128,4096]{1,0:T(8,128)S(1)}, u32[]{:S(2)}, u32[]{:S(2)}) %collective-permute-start.11) | collective-permute-done | bytes 2097184 | tf_op jit(solution)/shard_map/ppermute | solution.py:280
  552.1 64.4 %mlp.6 = (f32[128,4096]{1,0:T(8,128)}, f32[128,4096]{1,0:T(8,128)}, f32[64,4096]{1,0:T(8,128)}, f32[64,4096]{1,0:T(8,128)}, f32[128,4096]{1,0:T(8,128)}, /*index=5*/f32[16,4096]{1,0:T(8,128)}) custom-call(s32[1]{0:T(128)} %bitcast.place_ref, bf16[512,4096]{1,0:T(8,128)(2,1)} %copy-done.3, bf16[1,4096]{1,0:T(2,128)(2,1)} %gain_ref.7, ...), custom_call_target="tpu_custom_call" | custom-call | flops 45097156608 | bytes 88080384 | tf_op jit(solution)/shard_map/mlp/pallas_call | solution.py:260
  620.2 18.6 %collective-permute-done.17 = f32[64,4096]{1,0:T(8,128)S(1)} collective-permute-done((f32[64,4096]{1,0:T(8,128)}, f32[64,4096]{1,0:T(8,128)S(1)}, u32[]{:S(2)}, u32[]{:S(2)}) %collective-permute-start.17) | collective-permute-done | bytes 1048608 | tf_op jit(solution)/shard_map/ppermute | solution.py:280
  648.0 21.8 %project.7.h_ref = bf16[512,4096]{1,0:T(8,128)(2,1)S(1)} custom-call(s32[1]{0:T(128)} %bitcast.place_ref, bf16[4,512,1024]{2,1,0:T(8,128)(2,1)S(1)} %bitcast.83, bf16[4096,4096]{1,0:T(8,128)(2,1)} %all-gather.12.cloned.1.call-done.refs_5_.refs_1_, bf16[2048,4096]{1,0:T(8,128)(2,1)} %bitcast.92, bf16[2048,4096]{1,0:T(8,128)(2,1)} %bitcast.93), custom_call_target="tpu_custom_call" | custom-call | flops 17179869184 | bytes 33554432 | tf_op jit(solution)/shard_map/project/pallas_call | solution.py:179
  691.3 61.2 %mlp.7 = (f32[128,4096]{1,0:T(8,128)}, f32[128,4096]{1,0:T(8,128)}, f32[64,4096]{1,0:T(8,128)}, f32[64,4096]{1,0:T(8,128)}, f32[128,4096]{1,0:T(8,128)}) custom-call(s32[1]{0:T(128)} %bitcast.place_ref, bf16[512,4096]{1,0:T(8,128)(2,1)} %copy-done, bf16[1,4096]{1,0:T(2,128)(2,1)} %gain_ref.7, bf16[4096,3584]{1,0:T(8,128)(2,1)} %bitcast.112, ...), custom_call_target="tpu_custom_call" | custom-call | flops 45097156608 | bytes 88080384 | tf_op jit(solution)/shard_map/mlp/pallas_call | solution.py:260
  756.1 18.6 %collective-permute-done.21 = f32[64,4096]{1,0:T(8,128)S(1)} collective-permute-done((f32[64,4096]{1,0:T(8,128)}, f32[64,4096]{1,0:T(8,128)S(1)}, u32[]{:S(2)}, u32[]{:S(2)}) %collective-permute-start.21) | collective-permute-done | bytes 1048608 | tf_op jit(solution)/shard_map/ppermute | solution.py:280
  788.0 22.8 %collective-permute-done.26 = bf16[2,2048,128]{2,1,0:T(8,128)(2,1)S(1)} collective-permute-done((bf16[2,2048,128]{2,1,0:T(8,128)(2,1)}, bf16[2,2048,128]{2,1,0:T(8,128)(2,1)S(1)}, u32[]{:S(2)}, u32[]{:S(2)}) %collective-permute-start.26) | collective-permute-done | bytes 1048608 | tf_op jit(solution)/shard_map/ppermute | solution.py:337
  830.9 14.1 %collective-permute-done.22 = f32[128,4096]{1,0:T(8,128)} collective-permute-done((f32[128,4096]{1,0:T(8,128)}, f32[128,4096]{1,0:T(8,128)}, u32[]{:S(2)}, u32[]{:S(2)}) %collective-permute-start.22) | collective-permute-done | bytes 2097184 | tf_op jit(solution)/shard_map/ppermute | solution.py:280
  871.7 12.7 %broadcast_select_fusion = (bf16[1,1,16,512,2,128]{5,4,3,2,1,0:T(2,128)(2,1)}, bf16[1,1,16,512,2,128]{5,4,3,2,1,0:T(2,128)(2,1)}) fusion(bf16[1,1,16,512,2,128]{5,4,3,2,1,0:T(2,128)(2,1)S(1)} %copy-done.11, pred[16,512]{1,0:T(8,128)(4,1)S(1)} %copy-done.22, bf16[16,2,128]{2,1,0:T(2,128)(2,1)S(1)} %copy.37, ...), kind=kLoop, calls=%fused_computation.12 | loop fusion | flops 4194304 | bytes 16801792 | tf_op jit(solution)/shard_map/jit(_where)/select_n | solution.py:345
  (184 shorter events, 263.7 us)
Async XLA Ops:
  7.2 210.0 %all-gather.12.cloned.1.call-start = ((), (), s32[]{:S(2)}) async-start(), calls=%async_computation | async-start | bytes 34603008 | tf_op jit(solution)/shard_map/all_gather | solution.py:400
  9.7 293.4 %all-gather.22.cloned.1.call-start = ((), (), s32[]{:S(2)}) async-start(), calls=%async_computation.5 | async-start | bytes 5242880 | tf_op jit(solution)/shard_map/all_gather | solution.py:417
  109.3 384.5 %all-gather.24.cloned.1.call-start = ((), (), s32[]{:S(2)}) async-start(), calls=%async_computation.6 | async-start | bytes 5242880 | tf_op jit(solution)/shard_map/all_gather | solution.py:417
  138.5 507.3 %all-gather.26.cloned.1.call-start = ((), (), s32[]{:S(2)}) async-start(), calls=%async_computation.7 | async-start | bytes 5242880 | tf_op jit(solution)/shard_map/all_gather | solution.py:417
  172.6 711.8 %all-gather.14.cloned.1.call-start = ((), (), s32[]{:S(2)}) async-start(), calls=%async_computation.1 | async-start | bytes 5242880 | tf_op jit(solution)/shard_map/all_gather | solution.py:457
  312.1 49.5 %collective-permute-start.4 = (f32[64,4096]{1,0:T(8,128)}, f32[64,4096]{1,0:T(8,128)S(1)}, u32[]{:S(2)}, u32[]{:S(2)}) collective-permute-start(f32[64,4096]{1,0:T(8,128)} %get-tuple-element.45), channel_id=1, source_target_pairs={{0,8},{8,16},{16,24},{24,0},{1,9},{9,17},{17,25},{25,1},{2,10},{10... | collective-permute-start | bytes 3145736 | tf_op jit(solution)/shard_map/ppermute | solution.py:280
  357.9 69.4 %collective-permute-start.7 = (f32[128,4096]{1,0:T(8,128)}, f32[128,4096]{1,0:T(8,128)}, u32[]{:S(2)}, u32[]{:S(2)}) collective-permute-start(f32[128,4096]{1,0:T(8,128)} %add_dynamic-update-slice_fusion.6), channel_id=1, source_target_pairs={{8,0},{16,8},{24,16},{0,24},{9,1},{17,9},{25,17},{1,25},{10,2},{18... | collective-permute-start | bytes 6291464 | tf_op jit(solution)/shard_map/ppermute | solution.py:280
  364.1 63.3 %collective-permute-start.5 = (f32[128,4096]{1,0:T(8,128)}, f32[128,4096]{1,0:T(8,128)}, u32[]{:S(2)}, u32[]{:S(2)}) collective-permute-start(f32[128,4096]{1,0:T(8,128)} %add_dynamic-update-slice_fusion.7), channel_id=1, source_target_pairs={{0,8},{8,16},{16,24},{24,0},{1,9},{9,17},{17,25},{25,1},{2,10},{10... | collective-permute-start | bytes 6291464 | tf_op jit(solution)/shard_map/ppermute | solution.py:280
  431.5 460.3 %all-gather.16.cloned.1.call-start = ((), (), s32[]{:S(2)}) async-start(), calls=%async_computation.2 | async-start | bytes 5242880 | tf_op jit(solution)/shard_map/all_gather | solution.py:457
  434.6 47.2 %collective-permute-start.8 = (f32[64,4096]{1,0:T(8,128)}, f32[64,4096]{1,0:T(8,128)S(1)}, u32[]{:S(2)}, u32[]{:S(2)}) collective-permute-start(f32[64,4096]{1,0:T(8,128)} %get-tuple-element.53), channel_id=1, source_target_pairs={{0,8},{8,16},{16,24},{24,0},{1,9},{9,17},{17,25},{25,1},{2,10},{10... | collective-permute-start | bytes 3145736 | tf_op jit(solution)/shard_map/ppermute | solution.py:280
  439.3 44.8 %collective-permute-start.14 = (f32[1,16,4096]{2,1,0:T(8,128)S(1)}, f32[1,16,4096]{2,1,0:T(8,128)S(1)}, u32[]{:S(2)}, u32[]{:S(2)}) collective-permute-start(f32[1,16,4096]{2,1,0:T(8,128)S(1)} %fusion.13), channel_id=1, source_target_pairs={{8,0},{16,8},{24,16},{0,24},{9,1},{17,9},{25,17},{1,25},{10,2},{18... | collective-permute-start | bytes 786440 | tf_op jit(solution)/shard_map/ppermute | solution.py:280
  443.0 50.1 %collective-permute-start.13 = (f32[1,16,4096]{2,1,0:T(8,128)S(1)}, f32[1,16,4096]{2,1,0:T(8,128)S(1)}, u32[]{:S(2)}, u32[]{:S(2)}) collective-permute-start(f32[1,16,4096]{2,1,0:T(8,128)S(1)} %fusion.13), channel_id=1, source_target_pairs={{0,8},{8,16},{16,24},{24,0},{1,9},{9,17},{17,25},{25,1},{2,10},{10... | collective-permute-start | bytes 786440 | tf_op jit(solution)/shard_map/ppermute | solution.py:280
  443.0 50.1 %collective-permute-start.12 = (f32[1,16,4096]{2,1,0:T(8,128)S(1)}, f32[1,16,4096]{2,1,0:T(8,128)S(1)}, u32[]{:S(2)}, u32[]{:S(2)}) collective-permute-start(f32[1,16,4096]{2,1,0:T(8,128)S(1)} %fusion.13), channel_id=1, source_target_pairs={{0,16},{8,24},{16,0},{24,8},{1,17},{9,25},{17,1},{25,9},{2,18},{10... | collective-permute-start | bytes 786440 | tf_op jit(solution)/shard_map/ppermute | solution.py:318
  462.6 75.9 %collective-permute-start.11 = (f32[128,4096]{1,0:T(8,128)}, f32[128,4096]{1,0:T(8,128)S(1)}, u32[]{:S(2)}, u32[]{:S(2)}) collective-permute-start(f32[128,4096]{1,0:T(8,128)} %add_dynamic-update-slice_fusion.4), channel_id=1, source_target_pairs={{8,0},{16,8},{24,16},{0,24},{9,1},{17,9},{25,17},{1,25},{10,2},{18... | collective-permute-start | bytes 6291464 | tf_op jit(solution)/shard_map/ppermute | solution.py:280
  484.1 64.3 %collective-permute-start.9 = (f32[128,4096]{1,0:T(8,128)}, f32[128,4096]{1,0:T(8,128)}, u32[]{:S(2)}, u32[]{:S(2)}) collective-permute-start(f32[128,4096]{1,0:T(8,128)} %add_dynamic-update-slice_fusion.5), channel_id=1, source_target_pairs={{0,8},{8,16},{16,24},{24,0},{1,9},{9,17},{17,25},{25,1},{2,10},{10... | collective-permute-start | bytes 6291464 | tf_op jit(solution)/shard_map/ppermute | solution.py:280
  552.0 344.5 %all-gather.18.cloned.1.call-start = ((), (), s32[]{:S(2)}) async-start(), calls=%async_computation.3 | async-start | bytes 5242880 | tf_op jit(solution)/shard_map/all_gather | solution.py:457
  641.1 42.5 %collective-permute-start.18 = (f32[128,4096]{1,0:T(8,128)}, f32[128,4096]{1,0:T(8,128)S(1)}, u32[]{:S(2)}, u32[]{:S(2)}) collective-permute-start(f32[128,4096]{1,0:T(8,128)} %add_dynamic-update-slice_fusion.2), channel_id=1, source_target_pairs={{8,0},{16,8},{24,16},{0,24},{9,1},{17,9},{25,17},{1,25},{10,2},{18... | collective-permute-start | bytes 6291464 | tf_op jit(solution)/shard_map/ppermute | solution.py:280
  645.8 41.6 %collective-permute-start.16 = (f32[128,4096]{1,0:T(8,128)}, f32[128,4096]{1,0:T(8,128)}, u32[]{:S(2)}, u32[]{:S(2)}) collective-permute-start(f32[128,4096]{1,0:T(8,128)} %add_dynamic-update-slice_fusion.3), channel_id=1, source_target_pairs={{0,8},{8,16},{16,24},{24,0},{1,9},{9,17},{17,25},{25,1},{2,10},{10... | collective-permute-start | bytes 6291464 | tf_op jit(solution)/shard_map/ppermute | solution.py:280
  691.0 210.2 %all-gather.20.cloned.1.call-start = ((), (), s32[]{:S(2)}) async-start(), calls=%async_computation.4 | async-start | bytes 5242880 | tf_op jit(solution)/shard_map/all_gather | solution.py:457
  777.1 67.9 %collective-permute-start.22 = (f32[128,4096]{1,0:T(8,128)}, f32[128,4096]{1,0:T(8,128)}, u32[]{:S(2)}, u32[]{:S(2)}) collective-permute-start(f32[128,4096]{1,0:T(8,128)} %add_dynamic-update-slice_fusion), channel_id=1, source_target_pairs={{8,0},{16,8},{24,16},{0,24},{9,1},{17,9},{25,17},{1,25},{10,2},{18... | collective-permute-start | bytes 6291464 | tf_op jit(solution)/shard_map/ppermute | solution.py:280
  781.8 65.4 %collective-permute-start.20 = (f32[128,4096]{1,0:T(8,128)}, f32[128,4096]{1,0:T(8,128)}, u32[]{:S(2)}, u32[]{:S(2)}) collective-permute-start(f32[128,4096]{1,0:T(8,128)} %add_dynamic-update-slice_fusion.1), channel_id=1, source_target_pairs={{0,8},{8,16},{16,24},{24,0},{1,9},{9,17},{17,25},{25,1},{2,10},{10... | collective-permute-start | bytes 6291464 | tf_op jit(solution)/shard_map/ppermute | solution.py:280
  826.0 44.9 %collective-permute-start.24 = (f32[1,16,4096]{2,1,0:T(8,128)S(1)}, f32[1,16,4096]{2,1,0:T(8,128)S(1)}, u32[]{:S(2)}, u32[]{:S(2)}) collective-permute-start(f32[1,16,4096]{2,1,0:T(8,128)S(1)} %bitcast.98), channel_id=1, source_target_pairs={{0,8},{8,16},{16,24},{24,0},{1,9},{9,17},{17,25},{25,1},{2,10},{10... | collective-permute-start | bytes 786440 | tf_op jit(solution)/shard_map/ppermute | solution.py:280
  828.5 42.4 %collective-permute-start.25 = (f32[1,16,4096]{2,1,0:T(8,128)S(1)}, f32[1,16,4096]{2,1,0:T(8,128)S(1)}, u32[]{:S(2)}, u32[]{:S(2)}) collective-permute-start(f32[1,16,4096]{2,1,0:T(8,128)S(1)} %bitcast.99), channel_id=1, source_target_pairs={{8,0},{16,8},{24,16},{0,24},{9,1},{17,9},{25,17},{1,25},{10,2},{18... | collective-permute-start | bytes 786440 | tf_op jit(solution)/shard_map/ppermute | solution.py:280
  828.9 42.0 %collective-permute-start.23 = (f32[1,16,4096]{2,1,0:T(8,128)S(1)}, f32[1,16,4096]{2,1,0:T(8,128)S(1)}, u32[]{:S(2)}, u32[]{:S(2)}) collective-permute-start(f32[1,16,4096]{2,1,0:T(8,128)S(1)} %bitcast.100), channel_id=1, source_target_pairs={{0,16},{8,24},{16,0},{24,8},{1,17},{9,25},{17,1},{25,9},{2,18},{10... | collective-permute-start | bytes 786440 | tf_op jit(solution)/shard_map/ppermute | solution.py:318
  (41 other events, 1101.8 us)
Sparse Core Ops, SparseCore 0:
  10.1 110.2 all-gather.11
  122.5 58.0 all-gather.21
  182.2 56.0 all-gather.23
  239.8 45.9 all-gather.25
  431.6 85.7 all-gather.13
  552.1 46.2 all-gather.15
  691.1 46.3 all-gather.17
  852.0 46.1 all-gather.19
